TPU v7x, 128 devices: a whole 4x4x4 slice. The times are simulated.
128 devices in a mesh: ev: 8 (over z, core), mesh: 16 (over y, x).
Axes of the slice: x: 4, y: 4, z: 4, core: 2. Of those that a mesh axis runs over, the one named last changes fastest.
Arguments:
- kernels: bfloat16 [16, 12, 4096, 128], P('ev', None, 'mesh'), may hold values from -6 to 6
- tile_owner: int32 [16, 8192, 1], P('ev', 'mesh'), may hold values from 0 to 15; in each aligned block of 512 rows (0 to 511, 512 to 1023, ..., all dimensions but the last counted through in order) at most 64 rows name the same one
- tile_source: int32 [16, 8192], P('ev', 'mesh'), may hold values from 0 to 255
- tile_target: int32 [16, 8192], P('ev', 'mesh'), may hold values from 0 to 63
- tile_seed: int32 [16, 8192], P('ev', 'mesh'), may hold values from 0 to 83
- tile_count: int32 [16, 16], P('ev', 'mesh'), may hold values from 256 to 512
- prev_gradient: float32 [12, 16, 64, 128], P(None, 'mesh', 'ev'), may hold values from -18 to 18
- prev_step: float32 [12, 16, 64, 128], P(None, 'mesh', 'ev'), may hold values from -18 to 18, as said below
- precond: float32 [12, 16, 64, 128], P(None, 'mesh', 'ev'), may hold values from 0.2 to 2
Outputs:
- inversion_direction: float32 [12, 16, 64, 128], P(None, 'mesh', 'ev')
- event_direction: float32 [16, 12, 4096, 128], P('ev', None, 'mesh')
Inputs may be any that keep to these rules, and one draw needn't show every extreme that they name: `tile_owner`: in every aligned block of 512 rows (one event's list for one partition) no partition is named by more than 64 rows, a bound that some block reaches. Rows of a list at positions tile_count or later are padding. prev_step = -c * prev_gradient cell by cell, with c between 0.1 and 1.
All inputs are finite; a program needn't handle non-finite values.
Results may differ from a plain program's by a relative error of at most 0.0003.
The roundings to bfloat16 on the way count: a program that leaves them out, or rounds other values in their place, can miss the bound.
Values may be sent and summed in bfloat16 or wider, within the bound.
A program may use at most 128 MiB of HBM per device.

v0:
```python
import functools
import math

import jax
import jax.numpy as jnp
from jax import lax
from jax.sharding import Mesh
from jax.sharding import PartitionSpec as P

MESH = ("mesh_0", "mesh_1")
EV = ("ev_0", "ev_1")
EV_MESH = ("ev_0", "ev_1", "mesh_0", "mesh_1")


def split_up(array, dim, length):
    before, after = (array.shape[:dim], array.shape[dim + 1 :])
    return jnp.moveaxis(array.reshape(*before, length, -1, *after), dim, 0)


def summed_on_arrival(array, axis, dim):
    length = lax.axis_size(axis)
    parts = lax.all_to_all(split_up(array, dim, length), axis, 0, 0, tiled=True)
    return jnp.sum(parts, axis=0)


def over_axes(array, axes):
    return functools.reduce(lax.psum, axes, array)


def laid_out(parts, dim):
    shape = list(parts.shape[1:])
    shape[dim] *= parts.shape[0]
    return jnp.moveaxis(parts, 0, dim).reshape(shape)


def copy_for_each(array, axis):
    copies = jnp.broadcast_to(array, (lax.axis_size(axis), *array.shape))
    return lax.all_to_all(copies, axis, split_axis=0, concat_axis=0, tiled=True)


def collect(array, axis, dim):
    return laid_out(copy_for_each(array, axis), dim)


def make_tiles(seed_ids, node_count):
    node_pos = jnp.arange(node_count).astype(jnp.float32)
    offset = (seed_ids % 7 - 3).astype(jnp.float32)
    spread = 0.55 + 0.1 * (seed_ids // 7 % 3).astype(jnp.float32)
    weight = 0.1 + 0.1 * (seed_ids // 21).astype(jnp.float32)
    distance = node_pos[None, :, None] - node_pos[None, None, :] - offset[:, None, None]
    values = weight[:, None, None] * jnp.exp(
        -distance * distance / (2.0 * spread * spread)[:, None, None]
    )
    return values.astype(jnp.bfloat16)


def body(
    kernels,
    tile_owner,
    tile_source,
    tile_target,
    tile_seed,
    tile_count,
    prev_gradient,
    prev_step,
    precond,
):
    event_local, components, event_blocks, node_count = kernels.shape
    tiles_local = tile_source.shape[1]
    partitions = lax.axis_size(MESH)
    event_groups = lax.axis_size(EV)
    owned_blocks = precond.shape[2]
    sub_blocks = owned_blocks * event_groups
    capacity = tiles_local // 8
    total_tiles = event_local * tiles_local
    block_rows = math.gcd(total_tiles, 512)
    block_count = total_tiles // block_rows
    row_width = components * node_count
    list_pos = lax.broadcasted_iota(jnp.int32, (event_local, tiles_local), 1)
    event_of = lax.broadcasted_iota(jnp.int32, (event_local, tiles_local), 0).reshape(total_tiles)
    live_mask = (list_pos < tile_count).astype(jnp.float32).reshape(total_tiles)
    owner_ids = tile_owner.reshape(total_tiles)
    target_ids = tile_target.reshape(total_tiles)
    seed_ids = tile_seed.reshape(total_tiles)
    source_row = event_of * event_blocks + tile_source.reshape(total_tiles)
    kernel_rows = jnp.transpose(kernels, (0, 2, 1, 3)).reshape(
        event_local * event_blocks, components, node_count
    )

    def forward_block(inputs):
        block_seeds, block_rows_idx, block_live = inputs
        tile_mats = make_tiles(block_seeds, node_count)
        picked = kernel_rows[block_rows_idx]
        product = jnp.einsum("tcn,tnm->tcm", picked, tile_mats, preferred_element_type=jnp.float32)
        return (product * block_live[:, None, None]).astype(jnp.bfloat16)

    contribution = lax.map(
        forward_block,
        (
            seed_ids.reshape(block_count, block_rows),
            source_row.reshape(block_count, block_rows),
            live_mask.reshape(block_count, block_rows),
        ),
    )
    contribution = contribution.reshape(total_tiles, components, node_count)
    owner_hits = (
        owner_ids.reshape(event_local, tiles_local, 1)
        == jnp.arange(partitions, dtype=jnp.int32)[None, None, :]
    ).astype(jnp.float32)
    row_iota = lax.broadcasted_iota(jnp.int32, (tiles_local, tiles_local), 0)
    col_iota = lax.broadcasted_iota(jnp.int32, (tiles_local, tiles_local), 1)
    upper_ones = (row_iota <= col_iota).astype(jnp.float32)
    running = jnp.einsum("etp,ts->esp", owner_hits, upper_ones, precision=lax.Precision.HIGHEST)
    slot_index = (
        jnp.sum(owner_hits * (running - 1.0), axis=2).astype(jnp.int32).reshape(total_tiles)
    )
    slot_place = (owner_ids * event_local + event_of) * capacity + slot_index
    buffer_rows = partitions * event_local * capacity
    tile_number = jnp.arange(total_tiles, dtype=jnp.int32)
    slot_tile = jnp.zeros((buffer_rows,), jnp.int32).at[slot_place].set(tile_number + 1)
    slot_filled = slot_tile > 0
    fill_from = jnp.maximum(slot_tile - 1, 0)
    outgoing = jnp.where(
        slot_filled[:, None, None], contribution[fill_from], jnp.zeros((), jnp.bfloat16)
    )
    labels = jnp.where(slot_filled, target_ids[fill_from], 0)
    arrived, arrived_labels = (
        lax.all_to_all(
            outgoing.reshape(partitions, event_local * capacity, components, node_count),
            MESH,
            split_axis=0,
            concat_axis=0,
            tiled=True,
        ),
        lax.all_to_all(
            labels.reshape(partitions, event_local * capacity),
            MESH,
            split_axis=0,
            concat_axis=0,
            tiled=True,
        ),
    )
    flat_labels = arrived_labels.reshape(buffer_rows)
    label_hits = (jnp.arange(sub_blocks, dtype=jnp.int32)[:, None] == flat_labels[None, :]).astype(
        jnp.bfloat16
    )
    partial_sum = jnp.dot(
        label_hits, arrived.reshape(buffer_rows, row_width), preferred_element_type=jnp.float32
    ).reshape(sub_blocks, components, node_count)
    owned = summed_on_arrival(partial_sum, EV, 0)
    gradient = jnp.transpose(owned, (1, 0, 2))[:, None, :, :]
    change = gradient - prev_gradient
    weighted = precond * change
    curvature, slope, cross_term, self_term = (
        over_axes(jnp.sum(prev_step * change), EV_MESH),
        over_axes(jnp.sum(prev_step * gradient), EV_MESH),
        over_axes(jnp.sum(weighted * gradient), EV_MESH),
        over_axes(jnp.sum(weighted * change), EV_MESH),
    )
    alpha = slope / curvature
    scaled = precond * (gradient - alpha * change)
    bend = cross_term - alpha * self_term
    beta = bend / curvature
    inversion_direction = -(scaled + (alpha - beta) * prev_step)
    local_direction = jnp.transpose(inversion_direction.astype(jnp.bfloat16)[:, 0], (1, 0, 2))
    partition_rows = collect(local_direction, EV, 0)
    requested = jnp.einsum(
        "sr,sk->rk",
        label_hits,
        partition_rows.reshape(sub_blocks, row_width),
        preferred_element_type=jnp.float32,
    ).astype(jnp.bfloat16)
    returned = lax.all_to_all(
        requested.reshape(partitions, event_local * capacity, components, node_count),
        MESH,
        split_axis=0,
        concat_axis=0,
        tiled=True,
    )
    tile_rows = returned.reshape(buffer_rows, components, node_count)[slot_place]
    event_rows = event_local * event_blocks
    event_row_ids = jnp.arange(event_rows, dtype=jnp.int32)

    def backward_block(total, inputs):
        block_seeds, block_dirs, block_live, block_sources = inputs
        tile_mats = make_tiles(block_seeds, node_count)
        product = jnp.einsum(
            "tcm,tnm->tcn", block_dirs, tile_mats, preferred_element_type=jnp.float32
        )
        product = (product * block_live[:, None, None]).reshape(block_sources.shape[0], row_width)
        hits = (event_row_ids[:, None] == block_sources[None, :]).astype(jnp.float32)
        return (
            total
            + jnp.dot(
                hits, product, precision=lax.Precision.HIGHEST, preferred_element_type=jnp.float32
            ),
            None,
        )

    back_start = jnp.zeros((event_rows, row_width), jnp.float32)
    summed, _ = lax.scan(
        backward_block,
        back_start,
        (
            seed_ids.reshape(block_count, block_rows),
            tile_rows.reshape(block_count, block_rows, components, node_count),
            live_mask.reshape(block_count, block_rows),
            source_row.reshape(block_count, block_rows),
        ),
    )
    event_direction = jnp.transpose(
        summed.reshape(event_local, event_blocks, components, node_count), (0, 2, 1, 3)
    )
    return (inversion_direction, event_direction)


def solution(mesh):
    split = Mesh(mesh.devices.reshape(4, 2, 4, 4), ("ev_0", "ev_1", "mesh_0", "mesh_1"))
    in_specs = (
        P(EV, None, MESH, None),
        P(EV, MESH, None),
        P(EV, MESH),
        P(EV, MESH),
        P(EV, MESH),
        P(EV, MESH),
        P(None, MESH, EV, None),
        P(None, MESH, EV, None),
        P(None, MESH, EV, None),
    )
    out_specs = (P(None, MESH, EV, None), P(EV, None, MESH, None))
    return jax.shard_map(body, mesh=split, in_specs=in_specs, out_specs=out_specs, check_vma=False)
```

profile of v0, /device:TPU:1, one launch (start us, length us, event | category | flops | bytes accessed | tf_op | source)
XLA Modules:
  0.0 453.6 jit_solution(13637151153818595323)
XLA Ops:
  2.3 4.3 scatter_custom_fusion
  7.4 8.6 %gather_fusion.1 = s32[2048]{0:T(1024)S(1)} fusion(s32[1024]{0:T(1024)S(1)} %bitcast.139, s32[2048]{0:T(1024)S(1)} %maximum_clamp_fusion), kind=kCustom, calls=%fused_computation.1 | custom fusion | bytes 24576 | tf_op jit(solution)/shard_map/gather | solution.py:126
  19.2 29.2 %while.27 = (s32[]{:T(128)}, bf16[2,512,12,128]{3,2,1,0:T(8,128)(2,1)}, s32[2,512]{1,0:T(2,128)S(1)}, bf16[512,12,128]{2,1,0:T(8,128)(2,1)S(1)}, s32[2,512]{1,0:T(2,128)S(1)}, /*index=5*/f32[2,512]{1,0:T(2,128)S(1)}, s32[]{:T(128)}) while((s32[]{:T(128)}, bf16[2,512,12,128]{3,2,1,0:T(8,128)(2,1)}, s32[2,512]{1,0:T(2,128)S(1)}, ...), condition=%wide.region_3.4_spmd, body=%wide.region_2.3_spmd.sunk | while | flops 253268096 | bytes 7523933 | solution.py:97
  22.2 11.6 %fusion.79 = bf16[2,512,12,128]{3,2,1,0:T(8,128)(2,1)} fusion(bf16[2,512,12,128]{3,2,1,0:T(8,128)(2,1)} %get-tuple-element.459, s32[]{:T(128)} %get-tuple-element.458, f32[512]{0:T(512)S(1)} %bitcast.163, bf16[512,12,128]{2,1,0:T(8,128)(2,1)} %gather_fusion, f32[512]{0:T(512)S(1)} %get-tuple-element.435, f32[512]{0:T(512)S(1)} %fusion.78, ...), kind=kOutput, calls=%fused_computation.14.clone.1 | convolution fusion | flops 253231104 | bytes 4268544 | tf_op jit(solution)/shard_map/while/body/eval_jaxpr/tcn,tnm->tcm/dot_general | solution.py:94
  36.8 11.6 %fusion.79 = bf16[2,512,12,128]{3,2,1,0:T(8,128)(2,1)} fusion(bf16[2,512,12,128]{3,2,1,0:T(8,128)(2,1)} %get-tuple-element.459, s32[]{:T(128)} %get-tuple-element.458, f32[512]{0:T(512)S(1)} %bitcast.163, bf16[512,12,128]{2,1,0:T(8,128)(2,1)} %gather_fusion, f32[512]{0:T(512)S(1)} %get-tuple-element.435, f32[512]{0:T(512)S(1)} %fusion.78, ...), kind=kOutput, calls=%fused_computation.14.clone.1 | convolution fusion | flops 253231104 | bytes 4268544 | tf_op jit(solution)/shard_map/while/body/eval_jaxpr/tcn,tnm->tcm/dot_general | solution.py:94
  48.4 18.4 %gather_fusion.2 = bf16[2048,12,128]{2,1,0:T(8,128)(2,1)} fusion(bf16[1024,12,128]{2,1,0:T(8,128)(2,1)} %bitcast.145, s32[2048]{0:T(1024)S(1)} %copy-done.4), kind=kCustom, calls=%fused_computation.2 | custom fusion | bytes 12591104 | tf_op jit(solution)/shard_map/gather | solution.py:124
  66.8 5.0 %copy.46 = bf16[2048,12,128]{2,0,1:T(8,128)(2,1)S(1)} copy(bf16[2048,12,128]{2,1,0:T(8,128)(2,1)} %gather_fusion.2) | data formatting | bytes 12582912 | tf_op jit(solution)/shard_map/gather | solution.py:124
  75.1 8.7 %copy.47 = bf16[16,128,12,128]{1,3,2,0:T(8,128)(2,1)} copy(bf16[16,128,12,128]{3,1,0,2:T(8,128)(2,1)} %broadcast_select_fusion) | data formatting | bytes 12582912 | tf_op jit(solution)/shard_map/jit(_where)/select_n | solution.py:123
  83.8 79.9 %all_to_all.29 = bf16[16,128,12,128]{1,3,2,0:T(8,128)(2,1)} all-to-all(bf16[16,128,12,128]{1,3,2,0:T(8,128)(2,1)} %copy.47), channel_id=1, replica_groups=mesh['ev_0'=4,'ev_1'=2,'mesh_0'=4,'mesh_1'=4] {'mesh_0','mesh_1'}, dimensions={0} | all-to-all | bytes 12582912 | tf_op jit(solution)/shard_map/all_to_all | solution.py:128
  163.7 3.6 all-to-all-start
  167.3 7.7 %copy.48 = bf16[16,128,12,128]{1,0,3,2:T(8,128)(2,1)S(1)} copy(bf16[16,128,12,128]{1,3,2,0:T(8,128)(2,1)} %all_to_all.29) | data formatting | bytes 12582912 | tf_op jit(solution)/shard_map/all_to_all | solution.py:128
  175.0 5.9 %copy.64 = bf16[192,8,16,128]{3,1,2,0:T(8,128)(2,1)} copy(bf16[192,8,16,128]{3,2,1,0:T(8,128)(2,1)S(1)} %bitcast.143) | data formatting | bytes 12582912
  180.9 4.8 %fusion.45 = f32[8,8,12,128]{3,1,2,0:T(8,128)S(1)} fusion(bf16[12,128,2048,1]{2,1,0,3:T(8,128)(2,1)} %bitcast.147, s32[2048]{0:T(1024)S(1)} %bitcast.160, s32[8,8]{1,0:T(8,128)S(1)} %multiply_add_fusion.1), kind=kOutput, calls=%fused_computation.85 | convolution fusion | flops 402784256 | bytes 6693120 | tf_op jit(solution)/shard_map/dot_general | solution.py:147
  185.7 15.2 %all_to_all.30 = f32[8,8,12,128]{3,1,2,0:T(8,128)S(1)} all-to-all(f32[8,8,12,128]{3,1,2,0:T(8,128)S(1)} %fusion.45), channel_id=1, replica_groups=mesh['ev_0'=4,'ev_1'=2,'mesh_0'=4,'mesh_1'=4] {'ev_0','ev_1'}, dimensions={0} | all-to-all | bytes 786432 | tf_op jit(solution)/shard_map/all_to_all | solution.py:22
  201.6 7.6 %all-reduce.2 = (f32[]{:T(128)}, f32[]{:T(128)}, f32[]{:T(128)}, f32[]{:T(128)}) all-reduce(f32[]{:T(128)} %get-tuple-element.289, f32[]{:T(128)} %get-tuple-element.290, f32[]{:T(128)} %get-tuple-element.288, f32[]{:T(128)} %get-tuple-element.287), channel_id=1, replica_groups=mesh['ev_0'=4,'ev_1'=2,'mesh_0'=4,'mesh_1'=4] {'ev_0'}, use_global_device_ids=true, to_apply=%region_6.7 | all-reduce | flops 4 | bytes 32 | tf_op jit(solution)/shard_map/psum | solution.py:27
  209.2 5.7 %all-reduce.3 = (f32[]{:T(128)}, f32[]{:T(128)}, f32[]{:T(128)}, f32[]{:T(128)}) all-reduce(f32[]{:T(128)} %get-tuple-element.323, f32[]{:T(128)} %get-tuple-element.324, f32[]{:T(128)} %get-tuple-element.325, f32[]{:T(128)} %get-tuple-element.326), channel_id=1, replica_groups=mesh['ev_0'=4,'ev_1'=2,'mesh_0'=4,'mesh_1'=4] {'ev_1'}, use_global_device_ids=true, to_apply=%region_7.8 | all-reduce | flops 4 | bytes 32 | tf_op jit(solution)/shard_map/psum | solution.py:27
  214.9 9.3 %all-reduce.1 = (f32[]{:T(128)}, f32[]{:T(128)}, f32[]{:T(128)}, f32[]{:T(128)}) all-reduce(f32[]{:T(128)} %get-tuple-element.327, f32[]{:T(128)} %get-tuple-element.328, f32[]{:T(128)} %get-tuple-element.329, f32[]{:T(128)} %get-tuple-element.330), channel_id=1, replica_groups=mesh['ev_0'=4,'ev_1'=2,'mesh_0'=4,'mesh_1'=4] {'mesh_0'}, use_global_device_ids=true, to_apply=%region_8.9 | all-reduce | flops 4 | bytes 32 | tf_op jit(solution)/shard_map/psum | solution.py:27
  224.2 9.1 %all-reduce = (f32[]{:T(128)}, f32[]{:T(128)}, f32[]{:T(128)}, f32[]{:T(128)}) all-reduce(f32[]{:T(128)} %get-tuple-element.319, f32[]{:T(128)} %get-tuple-element.320, f32[]{:T(128)} %get-tuple-element.321, f32[]{:T(128)} %get-tuple-element.322), channel_id=1, replica_groups=mesh['ev_0'=4,'ev_1'=2,'mesh_0'=4,'mesh_1'=4] {'mesh_1'}, use_global_device_ids=true, to_apply=%region_9.10 | all-reduce | flops 4 | bytes 32 | tf_op jit(solution)/shard_map/psum | solution.py:27
  237.2 12.6 %all_to_all.31 = bf16[8,8,12,128]{3,1,2,0:T(8,128)(2,1)S(1)} all-to-all(bf16[8,8,12,128]{3,1,2,0:T(8,128)(2,1)S(1)} %broadcast_in_dim.67), channel_id=1, replica_groups=mesh['ev_0'=4,'ev_1'=2,'mesh_0'=4,'mesh_1'=4] {'ev_0','ev_1'}, dimensions={0} | all-to-all | bytes 393216 | tf_op jit(solution)/shard_map/all_to_all | solution.py:38
  249.9 4.6 %convolution_convert_fusion = bf16[2048,1536]{1,0:T(8,128)(2,1)} fusion(s32[2048]{0:T(1024)S(1)} %bitcast.161, bf16[8,8,12,128]{3,1,2,0:T(8,128)(2,1)S(1)} %all_to_all.31), kind=kOutput, calls=%fused_computation.79 | convolution fusion | flops 405929984 | bytes 6496256 | tf_op jit(solution)/shard_map/sr,sk->rk/dot_general | solution.py:167
  254.4 12.2 %reshape.487 = bf16[16,128,12,128]{3,2,1,0:T(8,128)(2,1)} reshape(bf16[2048,1536]{1,0:T(8,128)(2,1)} %convolution_convert_fusion) | data formatting | bytes 12582912 | tf_op jit(solution)/shard_map/reshape | solution.py:174
  266.6 12.1 %copy.50 = bf16[16,128,12,128]{1,3,2,0:T(8,128)(2,1)} copy(bf16[16,128,12,128]{3,2,1,0:T(8,128)(2,1)} %reshape.487) | data formatting | bytes 12582912 | tf_op jit(solution)/shard_map/reshape | solution.py:174
  278.7 4.8 %all-to-all-start.4 = ((bf16[16,128,12,128]{1,3,2,0:T(8,128)(2,1)}), bf16[16,128,12,128]{1,3,2,0:T(8,128)(2,1)}, u32[]{:S(2)}, u32[]{:S(2)}) async-start(bf16[16,128,12,128]{1,3,2,0:T(8,128)(2,1)} %copy.50), calls=%async_computation.4 | async-start | bytes 12582912 | tf_op jit(solution)/shard_map/all_to_all | solution.py:173
  283.5 92.4 %all-to-all-done.4 = bf16[16,128,12,128]{1,3,2,0:T(8,128)(2,1)} async-done(((bf16[16,128,12,128]{1,3,2,0:T(8,128)(2,1)}), bf16[16,128,12,128]{1,3,2,0:T(8,128)(2,1)}, u32[]{:S(2)}, u32[]{:S(2)}) %all-to-all-start.4) | async-done | bytes 6291488 | tf_op jit(solution)/shard_map/all_to_all | solution.py:173
  375.9 12.8 %copy.51 = bf16[16,128,12,128]{3,2,1,0:T(8,128)(2,1)} copy(bf16[16,128,12,128]{1,3,2,0:T(8,128)(2,1)} %all-to-all-done.4) | data formatting | bytes 12582912 | tf_op jit(solution)/shard_map/all_to_all | solution.py:173
  388.7 11.9 %gather_fusion.3 = bf16[1024,12,128]{2,1,0:T(8,128)(2,1)} fusion(bf16[2048,12,128]{2,1,0:T(8,128)(2,1)} %bitcast.144, s32[1024]{0:T(1024)S(1)} %broadcast_clamp_fusion), kind=kCustom, calls=%fused_computation.3 | custom fusion | bytes 6295552 | tf_op jit(solution)/shard_map/gather | solution.py:180
  400.6 41.6 %while.28 = (s32[]{:T(128)}, f32[512,1536]{1,0:T(8,128)}, s32[2,512]{1,0:T(2,128)S(1)}, bf16[2,512,12,128]{3,2,1,0:T(8,128)(2,1)}, s32[2,512]{1,0:T(2,128)S(1)}, /*index=5*/f32[2,512]{1,0:T(2,128)S(1)}, s32[]{:T(128)}, s32[]{:T(128)}) while((s32[]{:T(128)}, f32[512,1536]{1,0:T(8,128)}, s32[2,512]{1,0:T(2,128)S(1)}, ...), condition=%wide.region_26.27_spmd.clone, body=%wide.region_25.26_spmd.clone.sunk | while | flops 5086152192 | bytes 21149292 | solution.py:201
  400.8 12.0 %broadcast_multiply_fusion.3 = f32[512,12,128]{2,1,0:T(8,128)} fusion(f32[512]{0:T(512)S(1)} %bitcast.164, f32[512]{0:T(512)S(1)} %get-tuple-element.448, f32[512]{0:T(512)S(1)} %fusion.84, f32[128,128]{1,0:T(8,128)S(1)} %broadcast_subtract_fusion.5, f32[512]{0:T(512)S(1)} %get-tuple-element.449, bf16[2,512,12,128]{3,2,1,0:T(8,128)(2,1)} %get-tuple-element.491, ...), kind=kOutput, calls=%fused_computation.49.clone.1 | convolution fusion | flops 252444672 | bytes 5317120 | tf_op jit(solution)/shard_map/while/body/eval_jaxpr/tcm,tnm->tcn/dot_general | solution.py:187
  416.3 4.4 convolution_add_fusion.2
  420.9 12.0 %broadcast_multiply_fusion.3 = f32[512,12,128]{2,1,0:T(8,128)} fusion(f32[512]{0:T(512)S(1)} %bitcast.164, f32[512]{0:T(512)S(1)} %get-tuple-element.448, f32[512]{0:T(512)S(1)} %fusion.84, f32[128,128]{1,0:T(8,128)S(1)} %broadcast_subtract_fusion.5, f32[512]{0:T(512)S(1)} %get-tuple-element.449, bf16[2,512,12,128]{3,2,1,0:T(8,128)(2,1)} %get-tuple-element.491, ...), kind=kOutput, calls=%fused_computation.49.clone.1 | convolution fusion | flops 252444672 | bytes 5317120 | tf_op jit(solution)/shard_map/while/body/eval_jaxpr/tcm,tnm->tcn/dot_general | solution.py:187
  436.4 5.8 %convolution_add_fusion.2 = f32[512,1536]{1,0:T(8,128)} fusion(f32[512,1536]{0,1:T(8,128)S(1)} %bitcast.140, f32[512,1536]{1,0:T(8,128)} %get-tuple-element.481, pred[]{:T(512)S(6)} %compare.3, s32[512]{0:T(512)S(1)} %bitcast.159), kind=kOutput, calls=%fused_computation.47.clone.1 | convolution fusion | flops 4833673216 | bytes 9439233 | tf_op jit(solution)/shard_map/while/body/eval_jaxpr/dot_general | solution.py:194
  447.9 5.7 %copy.53 = f32[2,12,256,128]{3,2,1,0:T(8,128)} copy(f32[2,12,256,128]{2,0,3,1:T(2,128)} %bitcast.146) | data formatting | bytes 6291456
  (87 shorter events, 29.0 us)
Async XLA Ops:
  2.3 4.4 copy-start.6
  6.7 9.3 %copy-start.3 = (s32[2048]{0:T(1024)}, s32[2048]{0:T(1024)S(1)}, u32[]{:S(2)}) copy-start(s32[2048]{0:T(1024)S(1)} %maximum_clamp_fusion) | copy-start | bytes 24580
  7.4 9.2 %copy-start.10 = (s32[2,1]{0,1:T(1,128)S(1)}, s32[2,1]{0,1:T(1,128)}, u32[]{:S(2)}) copy-start(s32[2,1]{0,1:T(1,128)} %param.18) | copy-start | bytes 28
  7.4 9.3 %copy-start.9 = (s32[2,512]{1,0:T(2,128)S(1)}, s32[2,512]{1,0:T(2,128)}, u32[]{:S(2)}) copy-start(s32[2,512]{1,0:T(2,128)} %param.15) | copy-start | bytes 12292
  7.4 11.8 %copy-start = (s32[2,512]{1,0:T(2,128)S(1)}, s32[2,512]{1,0:T(2,128)}, u32[]{:S(2)}) copy-start(s32[2,512]{1,0:T(2,128)} %param.17) | copy-start | bytes 12292
  19.2 29.2 %copy-start.4 = (s32[2048]{0:T(1024)S(1)}, s32[2048]{0:T(1024)}, u32[]{:S(2)}) copy-start(s32[2048]{0:T(1024)} %copy-done.3) | copy-start | bytes 24580
  66.8 5.0 %copy-start.8 = (pred[2048]{0:T(1024)(128)(4,1)S(1)}, pred[2048]{0:T(1024)(128)(4,1)}, u32[]{:S(2)}) copy-start(pred[2048]{0:T(1024)(128)(4,1)} %get-tuple-element.335) | copy-start | bytes 6148
  163.7 17.2 %all-to-all-start = ((s32[16,1,128]{2,1,0:T(1,128)}), s32[16,1,128]{2,1,0:T(1,128)S(1)}, u32[]{:S(2)}, u32[]{:S(2)}) async-start(s32[16,1,128]{2,1,0:T(1,128)} %bitcast.13), calls=%async_computation | async-start | bytes 16384 | tf_op jit(solution)/shard_map/all_to_all | solution.py:135
  180.8 20.1 %copy-start.1 = (f32[12,1,8,128]{3,2,1,0:T(8,128)S(1)}, f32[12,1,8,128]{3,2,1,0:T(8,128)}, u32[]{:S(2)}) copy-start(f32[12,1,8,128]{3,2,1,0:T(8,128)} %param.20) | copy-start | bytes 147460
  180.8 20.1 %copy-start.2 = (f32[12,1,8,128]{3,2,1,0:T(8,128)S(1)}, f32[12,1,8,128]{3,2,1,0:T(8,128)}, u32[]{:S(2)}) copy-start(f32[12,1,8,128]{3,2,1,0:T(8,128)} %param.21) | copy-start | bytes 147460
  180.8 20.1 %copy-start.5 = (f32[12,1,8,128]{3,2,1,0:T(8,128)S(1)}, f32[12,1,8,128]{3,2,1,0:T(8,128)}, u32[]{:S(2)}) copy-start(f32[12,1,8,128]{3,2,1,0:T(8,128)} %param.19) | copy-start | bytes 147460
  278.7 4.8 %copy-start.7 = (s32[1024,1]{0,1:T(1,128)S(1)}, s32[1024,1]{0,1:T(1,128)}, u32[]{:S(2)}) copy-start(s32[1024,1]{0,1:T(1,128)} %copy-done.6) | copy-start | bytes 12292
  278.7 97.3 %all-to-all-start.4 = ((bf16[16,128,12,128]{1,3,2,0:T(8,128)(2,1)}), bf16[16,128,12,128]{1,3,2,0:T(8,128)(2,1)}, u32[]{:S(2)}, u32[]{:S(2)}) async-start(bf16[16,128,12,128]{1,3,2,0:T(8,128)(2,1)} %copy.50), calls=%async_computation.4 | async-start | bytes 12582912 | tf_op jit(solution)/shard_map/all_to_all | solution.py:173
where the time goes:
time: 456 us; the launch traced here: 454 us
  blocking collectives  139 us (30%)
  local copies, waits for them, and re-layouts  135 us (30%)
  waiting for transfers between devices  92.4 us (20%)
  matrix products  67.1 us (15%)
  starting transfers between devices  8.45 us (2%)
  other arithmetic  6.79 us (1%)
    all_to_all x1, waiting for transfers between devices, body(): lax.all_to_all(requested.reshape(partitions, event_local * capacity, comp...  92.4 us
    all_to_all x1, blocking collectives, body(): lax.all_to_all(outgoing.reshape(partitions, event_local * capacity, compo...  79.9 us
    psum x4, blocking collectives, over_axes(): return functools.reduce(lax.psum, axes, array)  31.7 us
    reshape x2, local copies, waits for them, and re-layouts, body(): requested.reshape(partitions, event_local * capacity, components, node_co...  24.2 us
    dot_general x2, matrix products, backward_block(): jnp.einsum('tcm,tnm->tcn', block_dirs, tile_mats, preferred_element_type=...  24.1 us
    gather x2, local copies, waits for them, and re-layouts, body(): contribution[fill_from]  23.4 us
    dot_general x2, matrix products, forward_block(): jnp.einsum('tcn,tnm->tcm', picked, tile_mats, preferred_element_type=jnp....  23.3 us
    all_to_all x1, blocking collectives, summed_on_arrival(): parts = lax.all_to_all(split_up(array, dim, length), axis, 0, 0, tiled=True)  15.2 us
  transfers between devices with their start and end apart: 2, of which 1 were waited for; matrix products, arithmetic and copies ran while one was open for 3% of the time, Pallas kernels for 0%

commit v1 on v0

v1 whole, which is shorter than its diff:
```python
import functools, math
import jax, jax.numpy as jnp
from jax import lax
from jax.experimental import pallas as pl
from jax.experimental.pallas import tpu as pltpu
from jax.sharding import PartitionSpec as P

C=12; N=128; E=256; T=512; V=2; S=84

def fill_tables(ext, table, flip):
    i = lax.broadcasted_iota(jnp.int32,(136,N),0).astype(jnp.float32) - 4.0
    j = lax.broadcasted_iota(jnp.int32,(136,N),1).astype(jnp.float32)
    d = i - j
    for sp in range(3):
        spread = jnp.float32(0.55) + jnp.float32(0.1)*jnp.float32(sp)
        e = jnp.exp(-d*d/(jnp.float32(2.0)*spread*spread))
        for wt in range(4):
            weight = jnp.float32(0.1)+jnp.float32(0.1)*jnp.float32(wt)
            ext[wt*3+sp] = weight*e
    for k in range(12):
        for o in range(7):
            off = o-3
            if flip: off = -off
            table[k*7+o] = ext[k, pl.ds(4-off,N),:].astype(jnp.bfloat16)

def fwd_kernel(code, k_ref, out_ref, ext, table, xs, scr):
    fill_tables(ext, table, False)
    for v in range(V):
        @pl.loop(0, E//16)
        def _(b):
            e0 = pl.multiple_of(b*16,16)
            for c in range(C):
                x = k_ref[v, c, pl.ds(e0,16), :].astype(jnp.float32)
                xs[pl.ds((v*E+e0)*C+c, 16, stride=C), :] = x
    U=16
    @pl.loop(0, V*T//U)
    def _(g):
        t0 = g*U
        for u in range(U):
            w = code[t0+u]
            seed = w & 127
            src = (w >> 7) & 511
            x = xs[pl.ds(src*C,16),:].astype(jnp.bfloat16)
            y = jnp.dot(x, table[seed], preferred_element_type=jnp.float32)
            scr[pl.ds(u*16,16),:] = y
        r0 = pl.multiple_of(t0,16)
        for c in range(C):
            out_ref[pl.ds(r0,U), c*N:(c+1)*N] = scr[pl.ds(c,U,stride=16),:].astype(jnp.bfloat16)

def forward(code, kern, cost=None):
    return pl.pallas_call(fwd_kernel,
        out_shape=jax.ShapeDtypeStruct((V*T, C*N), jnp.bfloat16),
        grid_spec=pltpu.PrefetchScalarGridSpec(num_scalar_prefetch=1, grid=(),
            in_specs=[pl.BlockSpec(memory_space=pltpu.VMEM)],
            out_specs=pl.BlockSpec(memory_space=pltpu.VMEM),
            scratch_shapes=[pltpu.VMEM((12,136,N),jnp.float32), pltpu.VMEM((S,N,N),jnp.bfloat16),
                pltpu.VMEM((V*E*C+16,N),jnp.float32), pltpu.VMEM((16*16,N),jnp.float32)]),
        compiler_params=pltpu.CompilerParams(vmem_limit_bytes=48<<20),
        name="fwd")(code, kern)

def bwd_kernel(code, d_ref, out_ref, ext, table, xs, acc0, acc1):
    fill_tables(ext, table, True)
    @pl.loop(0, 128)
    def _(b):
        xs[pl.ds(pl.multiple_of(b*96,96),96),:] = d_ref[b].astype(jnp.float32)
    zero = jnp.zeros((64,N),jnp.float32)
    @pl.loop(0, (E*C)//64)
    def _(b):
        acc0[pl.ds(pl.multiple_of(b*64,64),64),:] = zero
        acc1[pl.ds(pl.multiple_of(b*64,64),64),:] = zero
    U=8
    @pl.loop(0, T//U)
    def _(g):
        for u in range(U):
            for v in range(V):
                w = code[v*T+g*U+u]
                seed = w & 127
                dst = jnp.minimum(w >> 16, 1023)
                src = (w >> 7) & 255
                row = jnp.where((w >> 16) >= 1024, E*C, src*C)
                x = xs[pl.ds(dst*C,16),:].astype(jnp.bfloat16)
                y = jnp.dot(x, table[seed], preferred_element_type=jnp.float32)
                acc = (acc0,acc1)[v]
                acc[pl.ds(row,8),:] += y[:8]
                acc[pl.ds(row+8,4),:] += y[8:12]
    for v in range(V):
        acc = (acc0,acc1)[v]
        @pl.loop(0, E//8)
        def _(b):
            e0 = pl.multiple_of(b*8,8)
            for c in range(C):
                out_ref[v, c, pl.ds(e0,8), :] = acc[pl.ds(e0*C+c, 8, stride=C),:]

def backward(code, dirs):
    return pl.pallas_call(bwd_kernel,
        out_shape=jax.ShapeDtypeStruct((V, C, E, N), jnp.float32),
        grid_spec=pltpu.PrefetchScalarGridSpec(num_scalar_prefetch=1, grid=(),
            in_specs=[pl.BlockSpec(memory_space=pltpu.VMEM)],
            out_specs=pl.BlockSpec(memory_space=pltpu.VMEM),
            scratch_shapes=[pltpu.VMEM((12,136,N),jnp.float32), pltpu.VMEM((S,N,N),jnp.bfloat16),
                pltpu.VMEM((1024*C+16,N),jnp.float32), pltpu.VMEM((E*C+16,N),jnp.float32), pltpu.VMEM((E*C+16,N),jnp.float32)]),
        compiler_params=pltpu.CompilerParams(vmem_limit_bytes=48<<20),
        name="bwd")(code, dirs)


def body(kernels, tile_owner, tile_source, tile_target, tile_seed, tile_count, prev_gradient, prev_step, precond):
    pos = lax.broadcasted_iota(jnp.int32, (V, T), 1)
    live = pos < tile_count
    block = tile_owner.reshape(V, T) * 64 + tile_target
    src = tile_source + E * lax.broadcasted_iota(jnp.int32, (V, T), 0)
    block = jnp.where(live, block, 1024)
    code = (tile_seed + (src << 7) + (block << 16)).reshape(V * T)
    contribution = forward(code, kernels)
    hits = (jnp.arange(1024, dtype=jnp.int32)[:, None] == block.reshape(1, V * T)).astype(jnp.bfloat16)
    partial = jnp.dot(hits, contribution, preferred_element_type=jnp.float32)
    owned = lax.psum_scatter(partial, ("mesh", "ev"), scatter_dimension=0, tiled=True)
    gradient = jnp.transpose(owned.reshape(8, C, N), (1, 0, 2))[:, None]
    change = gradient - prev_gradient
    weighted = precond * change
    sums = jnp.stack([jnp.sum(prev_step * change), jnp.sum(prev_step * gradient), jnp.sum(weighted * gradient), jnp.sum(weighted * change)])
    curvature, slope, cross_term, self_term = lax.psum(sums, ("mesh", "ev"))
    alpha = slope / curvature
    scaled = precond * (gradient - alpha * change)
    beta = (cross_term - alpha * self_term) / curvature
    direction = -(scaled + (alpha - beta) * prev_step)
    local = jnp.transpose(direction.astype(jnp.bfloat16)[:, 0], (1, 0, 2)).reshape(1, 8 * C, N)
    dirs = lax.all_gather(local, ("mesh", "ev"), axis=0, tiled=True)
    return direction, backward(code, dirs)


def solution(mesh):
    in_specs = (
        P("ev", None, "mesh", None),
        P("ev", "mesh", None),
        P("ev", "mesh"),
        P("ev", "mesh"),
        P("ev", "mesh"),
        P("ev", "mesh"),
        P(None, "mesh", "ev", None),
        P(None, "mesh", "ev", None),
        P(None, "mesh", "ev", None),
    )
    out_specs = (P(None, "mesh", "ev", None), P("ev", None, "mesh", None))
    return jax.shard_map(body, mesh=mesh, in_specs=in_specs, out_specs=out_specs, check_vma=False)
```

time: 456 us -> 415 us (0.910)
  waiting for transfers between devices: 92.4 us -> 277 us
  local copies, waits for them, and re-layouts: 135 us -> 4.6 us
  blocking collectives: 139 us -> 64.6 us
  matrix products: 67.1 us -> 5.35 us
  Pallas kernels: 0 us -> 38.9 us
  between operations: 4.15 us -> 17.4 us
  starting transfers between devices: 8.45 us -> 0.08 us
    reduce_scatter x0 -> x1, waiting for transfers between devices: none -> 215 us  [body(): lax.psum_scatter(partial, ('mesh', 'ev'), scatter_dimension=0, tiled=True)]
    all_to_all x3 -> x0, blocking collectives: 108 us -> none  [the longest x1 79.9 us: body(): lax.all_to_all(outgoing.reshape(partitions, event_local * capacity, compo...]
    all_to_all x2 -> x0, waiting for transfers between devices: 92.4 us -> none  [the longest x1 92.4 us: body(): lax.all_to_all(requested.reshape(partitions, event_local * capacity, comp...]
    all_gather x0 -> x1, waiting for transfers between devices: none -> 62.8 us  [body(): dirs = lax.all_gather(local, ('mesh', 'ev'), axis=0, tiled=True)]
    dot_general x8 -> x1, matrix products: 66.9 us -> 5.35 us  [body(): partial = jnp.dot(hits, contribution, preferred_element_type=jnp.float32)]
    gather x6 -> x0, local copies, waits for them, and re-layouts: 49.3 us -> none  [the longest x2 23.4 us: body(): contribution[fill_from]]
    pallas_call x0 -> x2, Pallas kernels: none -> 38.9 us  [the longest x1 20.7 us: backward(): pl.pallas_call(bwd_kernel, out_shape=jax.ShapeDtypeStruct((V, C, E, N), j...]
    psum x4 -> x1, blocking collectives: 31.7 us -> 64.6 us  [body(): curvature, slope, cross_term, self_term = lax.psum(sums, ('mesh', 'ev'))]
  transfers between devices with their start and end apart: 2 -> 2, of which waited for: 1 -> 2; matrix products, arithmetic and copies ran while one was open for 3% -> 0% of each run, Pallas kernels for 0% -> 0%
where the time goes in v1:
time: 415 us
  waiting for transfers between devices  277 us (67%)
  blocking collectives  64.6 us (16%)
  Pallas kernels  38.9 us (9%)
  between operations  17.4 us (4%)
  other arithmetic  6.38 us (2%)
  matrix products  5.35 us (1%)
  local copies, waits for them, and re-layouts  4.6 us (1%)
    reduce_scatter x1, waiting for transfers between devices, body(): lax.psum_scatter(partial, ('mesh', 'ev'), scatter_dimension=0, tiled=True)  215 us
    psum x1, blocking collectives, body(): curvature, slope, cross_term, self_term = lax.psum(sums, ('mesh', 'ev'))  64.6 us
    all_gather x1, waiting for transfers between devices, body(): dirs = lax.all_gather(local, ('mesh', 'ev'), axis=0, tiled=True)  62.8 us
    pallas_call x1, Pallas kernels, backward(): pl.pallas_call(bwd_kernel, out_shape=jax.ShapeDtypeStruct((V, C, E, N), j...  20.7 us
    pallas_call x1, Pallas kernels, forward(): pl.pallas_call(fwd_kernel, out_shape=jax.ShapeDtypeStruct((V * T, C * N),...  18.3 us
  transfers between devices with their start and end apart: 2, of which 2 were waited for; matrix products, arithmetic and copies ran while one was open for 0% of the time, Pallas kernels for 0%

profile of v1, /device:TPU:1, one launch (start us, length us, event | category | flops | bytes accessed | tf_op | source)
XLA Modules:
  0.0 414.7 jit_solution(7072693435593310681)
XLA Ops:
  7.2 0.0 reduce-scatter.2.cloned.1.call-start
  7.2 0.8 add_bitcast_fusion
  8.1 0.0 copy-start.1
  8.1 1.4 copy-done.1
  9.5 18.3 %fwd.1 = bf16[1024,1536]{1,0:T(8,128)(2,1)S(1)} custom-call(s32[1024]{0:T(1024)S(1)} %bitcast.45, bf16[2,12,256,128]{3,2,1,0:T(8,128)(2,1)S(1)} %copy-done.1), custom_call_target="tpu_custom_call" | custom-call | tf_op jit(solution)/shard_map/fwd/pallas_call | solution.py:51
  27.7 5.4 %fusion = f32[1024,1536]{1,0:T(8,128)} fusion(bf16[1024,1536]{1,0:T(8,128)(2,1)S(1)} %fwd.1, s32[1024]{0:T(1024)S(1)} %bitcast.48), kind=kOutput, calls=%fused_computation.1 | convolution fusion | flops 3222274048 | bytes 9441280 | tf_op jit(solution)/shard_map/dot_general | solution.py:115
  33.1 0.0 copy-start.2
  33.1 0.0 copy-start.3
  33.1 0.0 copy-start.4
  33.1 0.0 reduce-scatter.2.cloned.1.call-update
  33.1 0.0 all-gather.2.cloned.1.call-start
  33.2 214.6 %reduce-scatter.2.cloned.1.call-done = f32[8,1536]{1,0:T(8,128)} async-done(((f32[1024,1536]{1,0:T(8,128)}), f32[8,1536]{1,0:T(8,128)}) %reduce-scatter.2.cloned.1.call-update) | async-done | bytes 49168 | tf_op jit(solution)/shard_map/reduce_scatter | solution.py:116
  247.7 0.0 copy-done.2
  247.7 0.0 copy-done.3
  247.7 0.0 copy-done.4
  247.8 1.5 fusion.3
  249.3 2.6 pad_maximum_fusion
  251.9 64.6 %psum.7 = f32[4]{0:T(128)S(1)} all-reduce(f32[4]{0:T(128)S(1)} %pad_maximum_fusion), channel_id=1, replica_groups=mesh['ev'=8,'mesh'=16] {'mesh','ev'}, use_global_device_ids=true, to_apply=%region_5.6 | all-reduce | flops 4 | bytes 32 | tf_op jit(solution)/shard_map/psum | solution.py:121
  316.5 0.7 fusion.8
  320.4 1.4 convert_bitcast_fusion
  321.9 0.6 reshape.20
  322.5 0.0 all-gather.2.cloned.1.call-update
  322.5 62.8 %all-gather.2.cloned.1.call-done.d_ref = bf16[128,96,128]{2,1,0:T(8,128)(2,1)} async-done(((bf16[1,96,128]{2,1,0:T(8,128)(2,1)}), bf16[128,96,128]{2,1,0:T(8,128)(2,1)}) %all-gather.2.cloned.1.call-update) | async-done | bytes 3145744 | tf_op jit(solution)/shard_map/all_gather | solution.py:127
  385.3 0.0 copy-start
  385.3 1.9 copy-done
  387.2 20.7 %bwd.1 = f32[2,12,256,128]{3,2,1,0:T(8,128)} custom-call(s32[1024]{0:T(1024)S(1)} %bitcast.46, bf16[128,96,128]{2,1,0:T(8,128)(2,1)S(1)} %copy-done), custom_call_target="tpu_custom_call" | custom-call | tf_op jit(solution)/shard_map/bwd/pallas_call | solution.py:95
  (4 shorter events, 0.0 us)
Async XLA Ops:
  7.2 240.6 %reduce-scatter.2.cloned.1.call-start = ((), (), s32[]{:S(2)}) async-start(), calls=%async_computation.1 | async-start | bytes 6340608 | tf_op jit(solution)/shard_map/reduce_scatter | solution.py:116
  8.1 1.4 copy-start.1
  33.1 214.7 %copy-start.2 = (f32[12,1,8,128]{3,2,1,0:T(8,128)S(1)}, f32[12,1,8,128]{3,2,1,0:T(8,128)}, u32[]{:S(2)}) copy-start(f32[12,1,8,128]{3,2,1,0:T(8,128)} %param.16) | copy-start | bytes 147460
  33.1 214.7 %copy-start.3 = (f32[12,1,8,128]{3,2,1,0:T(8,128)S(1)}, f32[12,1,8,128]{3,2,1,0:T(8,128)}, u32[]{:S(2)}) copy-start(f32[12,1,8,128]{3,2,1,0:T(8,128)} %param.17) | copy-start | bytes 147460
  33.1 214.7 %copy-start.4 = (f32[12,1,8,128]{3,2,1,0:T(8,128)S(1)}, f32[12,1,8,128]{3,2,1,0:T(8,128)}, u32[]{:S(2)}) copy-start(f32[12,1,8,128]{3,2,1,0:T(8,128)} %param.15) | copy-start | bytes 147460
  33.1 352.2 %all-gather.2.cloned.1.call-start = ((), (), s32[]{:S(2)}) async-start(), calls=%async_computation.2 | async-start | bytes 3170304 | tf_op jit(solution)/shard_map/all_gather | solution.py:127
  385.3 1.9 copy-start
Sparse Core Ops, SparseCore 0:
  33.2 214.4 reduce-scatter.1
  322.7 62.5 all-gather.1

commit v2 on v1

--- a/solution.py
+++ b/solution.py
@@ -60,9 +60,17 @@
 
 def bwd_kernel(code, d_ref, out_ref, ext, table, xs, acc0, acc1):
     fill_tables(ext, table, True)
-    @pl.loop(0, 128)
-    def _(b):
-        xs[pl.ds(pl.multiple_of(b*96,96),96),:] = d_ref[b].astype(jnp.float32)
+    for k in range(3):
+        a1, a2, a3 = AXES[k]
+        for rc in range(2):
+            @pl.loop(0, 64)
+            def _(b):
+                r = b >> 4
+                q = b & 15
+                base = r*WEIGHT[a1] + (q >> 2)*WEIGHT[a2] + (q & 3)*WEIGHT[a3] + rc*8
+                piece = d_ref[k, rc, r, q].astype(jnp.float32)
+                for cc in range(4):
+                    xs[pl.ds(base*C + k*4 + cc, 8, stride=C), :] = piece[cc*8:cc*8+8]
     zero = jnp.zeros((64,N),jnp.float32)
     @pl.loop(0, (E*C)//64)
     def _(b):
@@ -103,29 +111,219 @@
         name="bwd")(code, dirs)
 
 
+AXES = ((0, 1, 2), (1, 2, 0), (2, 0, 1))
+WEIGHT = (256, 64, 16)
+MESH_ID = pl.DeviceIdType.MESH
+
+
+def comm_kernel(code_ref, con_ref, pg_ref, ps_ref, pc_ref, dir_ref, tab_ref,
+                give, take, own, s1, s2, pr, row, rows,
+                gs, gr, s1s, s1r, s2s, s2r, ps, pr_sem, rs, rr, aps, apr, ars, arr, a2s, a2r, ads, adr):
+    e = lax.axis_index("ev")
+    m = lax.axis_index("mesh")
+    me = e * 16 + m
+    at = (lax.rem(m, 4), lax.div(m, 4), lax.div(e, 2))
+    core = lax.rem(e, 2)
+
+    def place(k, r, i, j, other=False):
+        off = [0, 0, 0]
+        for axis, o in zip(AXES[k], (r, i, j)):
+            off[axis] = o % 4
+        x, y, z = (lax.rem(a + o, 4) if o else a for a, o in zip(at, off))
+        return {"ev": z * 2 + (1 - core if other else core), "mesh": y * 4 + x}
+
+    def send(src, dst, ssem, rsem, where):
+        copy = pltpu.make_async_remote_copy(src_ref=src, dst_ref=dst, send_sem=ssem, recv_sem=rsem,
+                                            device_id=where, device_id_type=MESH_ID)
+        copy.start()
+
+    def got(ref, ssem, rsem):
+        pltpu.make_async_remote_copy(src_ref=ref, dst_ref=ref, send_sem=ssem, recv_sem=rsem,
+                                     device_id=place(0, 0, 0, 0, True), device_id_type=MESH_ID).wait_recv()
+
+    def sent(ref, ssem, rsem):
+        pltpu.make_async_remote_copy(src_ref=ref, dst_ref=ref, send_sem=ssem, recv_sem=rsem,
+                                     device_id=place(0, 0, 0, 0, True), device_id_type=MESH_ID).wait_send()
+
+    barrier = pltpu.get_barrier_semaphore()
+
+    def greet(d, carry):
+        other = lax.rem(me + d, 128)
+        pl.semaphore_signal(barrier, inc=1, device_id={"ev": lax.div(other, 16), "mesh": lax.rem(other, 16)},
+                            device_id_type=MESH_ID)
+        return carry
+
+    lax.fori_loop(1, 128, greet, 0)
+
+    ids = lax.broadcasted_iota(jnp.int32, (128, N), 0)
+    i_of, j_of, sub = ids >> 5, (ids >> 3) & 3, ids & 7
+    block = code_ref[...] >> 16
+
+    def partial(k, r, other):
+        a1, a2, a3 = AXES[k]
+        rows_k = i_of * WEIGHT[a2] + j_of * WEIGHT[a3] + sub
+        wanted = block - (r * WEIGHT[a1] + (8 if other else 0))
+        hits = jnp.concatenate([(rows_k == wanted[:, l * N:(l + 1) * N]).astype(jnp.float32).astype(jnp.bfloat16) for l in range(8)], axis=1)
+        return jnp.dot(hits, con_ref[:, k * 512:(k + 1) * 512], preferred_element_type=jnp.float32)
+
+    order = (2, 1, 3, 0)
+    for r in order:
+        for k in range(3):
+            got_k = partial(k, r, True)
+            for cc in range(4):
+                give[k, r, :, cc * 8:cc * 8 + 8, :] = got_k[:, cc * N:(cc + 1) * N].reshape(16, 8, N)
+            if r == 2 and k == 0:
+                pl.semaphore_wait(barrier, 127)
+            send(give.at[k, r], take.at[k, r], gs.at[k, r], gr.at[k, r], place(0, 0, 0, 0, True))
+    for r in order:
+        for k in range(3):
+            mine = partial(k, r, False)
+            got(take.at[k, r], gs.at[k, r], gr.at[k, r])
+            for cc in range(4):
+                own[k, r, :, cc * 8:cc * 8 + 8, :] = mine[:, cc * N:(cc + 1) * N].reshape(16, 8, N) + take[k, r, :, cc * 8:cc * 8 + 8, :]
+            up, down = place(k, 1, 0, 0), place(k, 3, 0, 0)
+            if r == 2:
+                send(own.at[k, 2, pl.ds(0, 8)], s1.at[k, 0], s1s.at[k, 0], s1r.at[k, 0], up)
+                send(own.at[k, 2, pl.ds(8, 8)], s1.at[k, 1], s1s.at[k, 1], s1r.at[k, 1], down)
+            if r == 1:
+                send(own.at[k, 1, pl.ds(8, 8)], s2.at[k, 0, pl.ds(8, 8)], s2s.at[k, 0, 1], s2r.at[k, 0, 1], up)
+            if r == 3:
+                send(own.at[k, 3, pl.ds(0, 8)], s2.at[k, 1, pl.ds(0, 8)], s2s.at[k, 1, 0], s2r.at[k, 1, 0], down)
+    for k in range(3):
+        up, down = place(k, 1, 0, 0), place(k, 3, 0, 0)
+        got(s1.at[k, 0], s1s.at[k, 0], s1r.at[k, 0])
+        own[k, 1, 0:8] = own[k, 1, 0:8] + s1[k, 0]
+        send(own.at[k, 1, pl.ds(0, 8)], s2.at[k, 0, pl.ds(0, 8)], s2s.at[k, 0, 0], s2r.at[k, 0, 0], up)
+        got(s1.at[k, 1], s1s.at[k, 1], s1r.at[k, 1])
+        own[k, 3, 8:16] = own[k, 3, 8:16] + s1[k, 1]
+        send(own.at[k, 3, pl.ds(8, 8)], s2.at[k, 1, pl.ds(8, 8)], s2s.at[k, 1, 1], s2r.at[k, 1, 1], down)
+    for k in range(3):
+        for way in range(2):
+            for half in range(2):
+                got(s2.at[k, way, pl.ds(half * 8, 8)], s2s.at[k, way, half], s2r.at[k, way, half])
+        own[k, 0] = own[k, 0] + s2[k, 0] + s2[k, 1]
+        for q in range(1, 16):
+            send(own.at[k, 0, q], pr.at[k, q - 1], ps.at[k], pr_sem.at[k], place(k, 0, q // 4, q % 4))
+    parts = []
+    for k in range(3):
+        got(pr.at[k], ps.at[k], pr_sem.at[k])
+        total = own[k, 0, 0]
+        for q in range(15):
+            total = total + pr[k, q]
+        parts.append(total)
+    gradient = jnp.concatenate(parts, axis=0)
+    prev_g = pg_ref[...].reshape(96, N)
+    step = ps_ref[...].reshape(96, N)
+    cond = pc_ref[...].reshape(96, N)
+    change = gradient - prev_g
+    weighted = cond * change
+    lane = lax.broadcasted_iota(jnp.int32, (1, N), 1)
+
+    def summed(v):
+        v = jnp.sum(v.reshape(12, 8, N), axis=0)
+        return jnp.sum(jnp.sum(v, axis=0, keepdims=True), axis=1, keepdims=True)
+
+    mine = jnp.zeros((1, N), jnp.float32)
+    for n, v in enumerate((step * change, step * gradient, weighted * gradient, weighted * change)):
+        mine = jnp.where(lane == n, summed(v), mine)
+    row[...] = mine
+    rows[me] = mine
+
+    def tell(d, carry):
+        other = lax.rem(me + d, 128)
+        send(row, rows.at[me], rs, rr, {"ev": lax.div(other, 16), "mesh": lax.rem(other, 16)})
+        return carry
+
+    lax.fori_loop(1, 128, tell, 0)
+    got(rows.at[pl.ds(0, 127)], rs, rr)
+    totals = jnp.sum(rows[...], axis=0)
+    curvature, slope, cross, self_ = (
+        jnp.sum(jnp.where(lane == n, totals, 0.0), axis=1, keepdims=True) for n in range(4))
+    alpha = slope / curvature
+    beta = (cross - alpha * self_) / curvature
+    scaled = cond * (gradient - alpha * change)
+    direction = -(scaled + (alpha - beta) * step)
+    dir_ref[...] = direction.reshape(12, 1, 8, N)
+    rounded = direction.astype(jnp.bfloat16)
+    partner = place(0, 0, 0, 0, True)
+    for k in range(3):
+        tab_ref[k, 0, 0, 0] = rounded[k * 32:(k + 1) * 32]
+    for k in range(3):
+        for q in range(1, 16):
+            i, j = q // 4, q % 4
+            back = (-i % 4) * 4 + (-j % 4)
+            send(tab_ref.at[k, 0, 0, 0], tab_ref.at[k, 0, 0, back], aps.at[k], apr.at[k], place(k, 0, i, j))
+    for k in range(3):
+        got(tab_ref.at[k, 0, 0, pl.ds(1, 15)], aps.at[k], apr.at[k])
+        send(tab_ref.at[k, 0, 0], tab_ref.at[k, 0, 3], ars.at[k, 0], arr.at[k, 0], place(k, 1, 0, 0))
+        send(tab_ref.at[k, 0, 0], tab_ref.at[k, 0, 1], ars.at[k, 1], arr.at[k, 1], place(k, 3, 0, 0))
+        send(tab_ref.at[k, 0, 0], tab_ref.at[k, 1, 0], ads.at[k, 0], adr.at[k, 0], partner)
+    for k in range(3):
+        got(tab_ref.at[k, 0, 3], ars.at[k, 0], arr.at[k, 0])
+        send(tab_ref.at[k, 0, 3, pl.ds(0, 8)], tab_ref.at[k, 0, 2, pl.ds(0, 8)], a2s.at[k, 0], a2r.at[k, 0], place(k, 1, 0, 0))
+        send(tab_ref.at[k, 0, 3], tab_ref.at[k, 1, 3], ads.at[k, 3], adr.at[k, 3], partner)
+        got(tab_ref.at[k, 0, 1], ars.at[k, 1], arr.at[k, 1])
+        send(tab_ref.at[k, 0, 1, pl.ds(8, 8)], tab_ref.at[k, 0, 2, pl.ds(8, 8)], a2s.at[k, 1], a2r.at[k, 1], place(k, 3, 0, 0))
+        send(tab_ref.at[k, 0, 1], tab_ref.at[k, 1, 1], ads.at[k, 1], adr.at[k, 1], partner)
+    for k in range(3):
+        got(tab_ref.at[k, 0, 2, pl.ds(0, 8)], a2s.at[k, 0], a2r.at[k, 0])
+        got(tab_ref.at[k, 0, 2, pl.ds(8, 8)], a2s.at[k, 1], a2r.at[k, 1])
+        send(tab_ref.at[k, 0, 2], tab_ref.at[k, 1, 2], ads.at[k, 2], adr.at[k, 2], partner)
+    for k in range(3):
+        for r in range(4):
+            got(tab_ref.at[k, 1, r], ads.at[k, r], adr.at[k, r])
+    for k in range(3):
+        for r in range(4):
+            sent(give.at[k, r], gs.at[k, r], gr.at[k, r])
+            sent(tab_ref.at[k, 0, r], ads.at[k, r], adr.at[k, r])
+        for way in range(2):
+            sent(s1.at[k, way], s1s.at[k, way], s1r.at[k, way])
+            for half in range(2):
+                sent(s2.at[k, way, pl.ds(half * 8, 8)], s2s.at[k, way, half], s2r.at[k, way, half])
+            sent(tab_ref.at[k, 0, 0], ars.at[k, way], arr.at[k, way])
+            sent(tab_ref.at[k, 0, 0, pl.ds(0, 8)], a2s.at[k, way], a2r.at[k, way])
+        sent(pr.at[k], ps.at[k], pr_sem.at[k])
+        sent(tab_ref.at[k, 0, 0, pl.ds(1, 15)], aps.at[k], apr.at[k])
+    sent(rows.at[pl.ds(0, 127)], rs, rr)
+
+
+def exchange(code, contribution, prev_gradient, prev_step, precond):
+    dma = pltpu.SemaphoreType.DMA
+    f32 = jnp.float32
+    pairs = [dma((3, 4)), dma((3, 2)), dma((3, 2, 2)), dma((3,)), dma, dma((3,)), dma((3, 2)), dma((3, 2)), dma((3, 4))]
+    return pl.pallas_call(
+        comm_kernel,
+        out_shape=(jax.ShapeDtypeStruct((C, 1, 8, N), f32), jax.ShapeDtypeStruct((3, 2, 4, 16, 32, N), jnp.bfloat16)),
+        in_specs=[pl.BlockSpec(memory_space=pltpu.VMEM)] * 5,
+        out_specs=(pl.BlockSpec(memory_space=pltpu.VMEM), pl.BlockSpec(memory_space=pltpu.VMEM)),
+        scratch_shapes=[
+            pltpu.VMEM((3, 4, 16, 32, N), f32), pltpu.VMEM((3, 4, 16, 32, N), f32), pltpu.VMEM((3, 4, 16, 32, N), f32),
+            pltpu.VMEM((3, 2, 8, 32, N), f32), pltpu.VMEM((3, 2, 16, 32, N), f32), pltpu.VMEM((3, 15, 32, N), f32),
+            pltpu.VMEM((1, N), f32), pltpu.VMEM((128, 1, N), f32),
+        ] + [p for p in pairs for _ in range(2)],
+        compiler_params=pltpu.CompilerParams(vmem_limit_bytes=48 << 20, collective_id=0, has_side_effects=True),
+        name="exchange",
+    )(code, contribution, prev_gradient, prev_step, precond)
+
+
 def body(kernels, tile_owner, tile_source, tile_target, tile_seed, tile_count, prev_gradient, prev_step, precond):
     pos = lax.broadcasted_iota(jnp.int32, (V, T), 1)
     live = pos < tile_count
-    block = tile_owner.reshape(V, T) * 64 + tile_target
+    m = lax.axis_index("mesh")
+    e = lax.axis_index("ev")
+    owner = tile_owner.reshape(V, T)
+    x = ((owner & 3) - (m & 3)) & 3
+    y = ((owner >> 2) - (m >> 2)) & 3
+    z = ((tile_target >> 4) - (e >> 1)) & 3
+    c = (tile_target >> 3) ^ e
+    block = x * 256 + y * 64 + z * 16 + (c & 1) * 8 + (tile_target & 7)
     src = tile_source + E * lax.broadcasted_iota(jnp.int32, (V, T), 0)
     block = jnp.where(live, block, 1024)
-    code = (tile_seed + (src << 7) + (block << 16)).reshape(V * T)
-    contribution = forward(code, kernels)
-    hits = (jnp.arange(1024, dtype=jnp.int32)[:, None] == block.reshape(1, V * T)).astype(jnp.bfloat16)
-    partial = jnp.dot(hits, contribution, preferred_element_type=jnp.float32)
-    owned = lax.psum_scatter(partial, ("mesh", "ev"), scatter_dimension=0, tiled=True)
-    gradient = jnp.transpose(owned.reshape(8, C, N), (1, 0, 2))[:, None]
-    change = gradient - prev_gradient
-    weighted = precond * change
-    sums = jnp.stack([jnp.sum(prev_step * change), jnp.sum(prev_step * gradient), jnp.sum(weighted * gradient), jnp.sum(weighted * change)])
-    curvature, slope, cross_term, self_term = lax.psum(sums, ("mesh", "ev"))
-    alpha = slope / curvature
-    scaled = precond * (gradient - alpha * change)
-    beta = (cross_term - alpha * self_term) / curvature
-    direction = -(scaled + (alpha - beta) * prev_step)
-    local = jnp.transpose(direction.astype(jnp.bfloat16)[:, 0], (1, 0, 2)).reshape(1, 8 * C, N)
-    dirs = lax.all_gather(local, ("mesh", "ev"), axis=0, tiled=True)
-    return direction, backward(code, dirs)
+    code = tile_seed + (src << 7) + (block << 16)
+    flat = code.reshape(V * T)
+    contribution = forward(flat, kernels)
+    direction, table = exchange(code.reshape(1, V * T), contribution, prev_gradient, prev_step, precond)
+    return direction, backward(flat, table)
 
 
 def solution(mesh):

time: 415 us -> 108 us (0.26)
  waiting for transfers between devices: 277 us -> 0 us
  blocking collectives: 64.6 us -> 0 us
  Pallas kernels: 38.9 us -> 102 us
  between operations: 17.4 us -> 0.69 us
  other arithmetic: 6.38 us -> 0.82 us
  matrix products: 5.35 us -> 0 us
    reduce_scatter x1 -> x0, waiting for transfers between devices: 215 us -> none  [body(): lax.psum_scatter(partial, ('mesh', 'ev'), scatter_dimension=0, tiled=True)]
    psum x1 -> x0, blocking collectives: 64.6 us -> none  [body(): curvature, slope, cross_term, self_term = lax.psum(sums, ('mesh', 'ev'))]
    all_gather x1 -> x0, waiting for transfers between devices: 62.8 us -> none  [body(): dirs = lax.all_gather(local, ('mesh', 'ev'), axis=0, tiled=True)]
    pallas_call x0 -> x1, Pallas kernels: none -> 60.7 us  [exchange(): pl.pallas_call(comm_kernel, out_shape=(jax.ShapeDtypeStruct((C, 1, 8, N),...]
    dot_general x1 -> x0, matrix products: 5.35 us -> none  [body(): partial = jnp.dot(hits, contribution, preferred_element_type=jnp.float32)]
  transfers between devices with their start and end apart: 2 -> 0, of which waited for: 2 -> 0; matrix products, arithmetic and copies ran while one was open for 0% -> 0% of each run, Pallas kernels for 0% -> 0%
where the time goes in v2:
time: 108 us; the launch traced here: 107 us
  Pallas kernels  102 us (94%)
  local copies, waits for them, and re-layouts  3.71 us (3%)
    pallas_call x1, Pallas kernels, exchange(): pl.pallas_call(comm_kernel, out_shape=(jax.ShapeDtypeStruct((C, 1, 8, N),...  60.7 us
    pallas_call x1, Pallas kernels, backward(): pl.pallas_call(bwd_kernel, out_shape=jax.ShapeDtypeStruct((V, C, E, N), j...  23.2 us
    pallas_call x1, Pallas kernels, forward(): pl.pallas_call(fwd_kernel, out_shape=jax.ShapeDtypeStruct((V * T, C * N),...  18.3 us
    unnamed x13, local copies, waits for them, and re-layouts  3.71 us

profile of v2, /device:TPU:1, one launch (start us, length us, event | category | flops | bytes accessed | tf_op | source)
XLA Modules:
  0.0 107.4 jit_solution(13364082677291442757)
XLA Ops:
  0.6 0.0 copy-start.2
  0.7 0.8 fusion.1
  1.5 0.0 copy-start.1
  1.5 1.4 %copy-done.1 = bf16[2,12,256,128]{3,2,1,0:T(8,128)(2,1)S(1)} copy-done((bf16[2,12,256,128]{3,2,1,0:T(8,128)(2,1)S(1)}, bf16[2,12,256,128]{3,2,1,0:T(8,128)(2,1)}, u32[]{:S(2)}) %copy-start.1) | copy-done | bytes 1572888
  2.9 0.0 copy-start.3
  2.9 0.0 copy-start.4
  2.9 18.3 %fwd.1.con_ref = bf16[1024,1536]{1,0:T(8,128)(2,1)S(1)} custom-call(s32[1024]{0:T(1024)S(1)} %bitcast.14, bf16[2,12,256,128]{3,2,1,0:T(8,128)(2,1)S(1)} %copy-done.1), custom_call_target="tpu_custom_call" | custom-call | tf_op jit(solution)/shard_map/fwd/pallas_call | solution.py:51
  21.2 0.0 copy-start
  21.2 1.7 %copy-done = bf16[1024,1536]{1,0:T(8,128)(2,1)} copy-done((bf16[1024,1536]{1,0:T(8,128)(2,1)}, bf16[1024,1536]{1,0:T(8,128)(2,1)S(1)}, u32[]{:S(2)}) %copy-start) | copy-done | bytes 3145752
  22.9 0.0 copy-done.2
  22.9 0.0 copy-done.3
  22.9 0.0 copy-done.4
  22.9 60.7 %exchange.1 = (f32[12,1,8,128]{3,2,1,0:T(8,128)S(1)}, bf16[3,2,4,16,32,128]{5,4,3,2,1,0:T(8,128)(2,1)S(1)}) custom-call(s32[1,1024]{1,0:T(1,128)S(1)} %bitcast.16, bf16[1024,1536]{1,0:T(8,128)(2,1)} %copy-done, f32[12,1,8,128]{3,2,1,0:T(8,128)S(1)} %copy-done.2, f32[12,1,8,128]{3,2,1,0:T(8,128)S(1)} %copy-done.3, f32[12,1,8,128]{3,2,1,0:T(8,128)S(1)} %copy-done.4), custom_call_target="tpu_custom_call" | custom-call | tf_op jit(solution)/shard_map/exchange/pallas_call | solution.py:294
  83.6 23.2 %bwd.1 = f32[2,12,256,128]{3,2,1,0:T(8,128)} custom-call(s32[1024]{0:T(1024)S(1)} %bitcast.15, bf16[3,2,4,16,32,128]{5,4,3,2,1,0:T(8,128)(2,1)S(1)} %get-tuple-element.5.d_ref), custom_call_target="tpu_custom_call" | custom-call | tf_op jit(solution)/shard_map/bwd/pallas_call | solution.py:103
  106.8 0.6 copy.17
  (3 shorter events, 0.0 us)
Async XLA Ops:
  0.6 22.2 %copy-start.2 = (f32[12,1,8,128]{3,2,1,0:T(8,128)S(1)}, f32[12,1,8,128]{3,2,1,0:T(8,128)}, u32[]{:S(2)}) copy-start(f32[12,1,8,128]{3,2,1,0:T(8,128)} %pg_ref.1) | copy-start | bytes 147460
  1.5 1.4 %copy-start.1 = (bf16[2,12,256,128]{3,2,1,0:T(8,128)(2,1)S(1)}, bf16[2,12,256,128]{3,2,1,0:T(8,128)(2,1)}, u32[]{:S(2)}) copy-start(bf16[2,12,256,128]{3,2,1,0:T(8,128)(2,1)} %k_ref.1) | copy-start | bytes 4718596
  2.9 20.0 %copy-start.3 = (f32[12,1,8,128]{3,2,1,0:T(8,128)S(1)}, f32[12,1,8,128]{3,2,1,0:T(8,128)}, u32[]{:S(2)}) copy-start(f32[12,1,8,128]{3,2,1,0:T(8,128)} %ps_ref.1) | copy-start | bytes 147460
  2.9 20.0 %copy-start.4 = (f32[12,1,8,128]{3,2,1,0:T(8,128)S(1)}, f32[12,1,8,128]{3,2,1,0:T(8,128)}, u32[]{:S(2)}) copy-start(f32[12,1,8,128]{3,2,1,0:T(8,128)} %pc_ref.1) | copy-start | bytes 147460
  21.2 1.7 %copy-start = (bf16[1024,1536]{1,0:T(8,128)(2,1)}, bf16[1024,1536]{1,0:T(8,128)(2,1)S(1)}, u32[]{:S(2)}) copy-start(bf16[1024,1536]{1,0:T(8,128)(2,1)S(1)} %fwd.1.con_ref) | copy-start | bytes 9437188

commit v3 on v1

v3 whole, which is shorter than its diff:
```python
import jax
import jax.numpy as jnp
from jax import lax
from jax.experimental import pallas as pl
from jax.experimental.pallas import tpu as pltpu
from jax.sharding import PartitionSpec as P

C, N, E, T, V, S = 12, 128, 256, 512, 2, 84
TILES = V * T
AXES = ((0, 1, 2), (1, 2, 0), (2, 0, 1))
WEIGHT = (256, 64, 16)
HOPS = (0, 1, 2, 1)
MESH_ID = pl.DeviceIdType.MESH
FWD_UNROLL = 64
BWD_UNROLL = 64


def fill_tables(ext, table, flip):
    i = lax.broadcasted_iota(jnp.int32, (136, N), 0).astype(jnp.float32) - 4.0
    j = lax.broadcasted_iota(jnp.int32, (136, N), 1).astype(jnp.float32)
    d = i - j
    for sp in range(3):
        spread = jnp.float32(0.55) + jnp.float32(0.1) * jnp.float32(sp)
        e = jnp.exp(-d * d / (jnp.float32(2.0) * spread * spread))
        for wt in range(4):
            weight = jnp.float32(0.1) + jnp.float32(0.1) * jnp.float32(wt)
            ext[wt * 3 + sp] = weight * e
    for k in range(12):
        for o in range(7):
            off = 3 - o if flip else o - 3
            table[k * 7 + o] = ext[k, pl.ds(4 - off, N), :].astype(jnp.bfloat16)


def main_kernel(code_s, code_ref, kern_hbm, pg_hbm, ps_hbm, pc_hbm, dir_ref, out_ref,
                kern, fields, ext, table, xs, scr, con, give, take, own, s1, s2, pr, row, rows, tab,
                kern_sem, field_sem, g_s, s1_s, s2_s, p_s, r_s, ap_s, ar_s, a2_s, ad_s,
                g_r, s1_r, s2_r, p_r, r_r, ap_r, ar_r, a2_r, ad_r):
    e = lax.axis_index("ev")
    m = lax.axis_index("mesh")
    me = e * 16 + m
    at = (lax.rem(m, 4), lax.div(m, 4), lax.div(e, 2))
    core = lax.rem(e, 2)
    coord = [[a if o == 0 else lax.rem(a + o, 4) for o in range(4)] for a in at]

    def device(dx, dy, dz, other=False):
        c = 1 - core if other else core
        return {"ev": coord[2][dz] * 2 + c, "mesh": coord[1][dy] * 4 + coord[0][dx]}

    def place(k, r, i, j):
        off = [0, 0, 0]
        for axis, o in zip(AXES[k], (r, i, j)):
            off[axis] = o % 4
        return device(*off)

    partner = device(0, 0, 0, True)

    def copy(src, dst, ssem, rsem, where):
        return pltpu.make_async_remote_copy(src_ref=src, dst_ref=dst, send_sem=ssem, recv_sem=rsem,
                                            device_id=where, device_id_type=MESH_ID)

    def send(src, dst, ssem, rsem, where):
        copy(src, dst, ssem, rsem, where).start()

    def got(ref, ssem, rsem):
        copy(ref, ref, ssem, rsem, partner).wait_recv()

    def sent(ref, ssem, rsem):
        copy(ref, ref, ssem, rsem, partner).wait_send()

    load = pltpu.make_async_copy(kern_hbm, kern, kern_sem)
    load.start()
    loads = [pltpu.make_async_copy(src, fields.at[n], field_sem.at[n]) for n, src in enumerate((pg_hbm, ps_hbm, pc_hbm))]
    for one in loads:
        one.start()
    barrier = pltpu.get_barrier_semaphore()

    def greet(d, carry):
        other = lax.rem(me + d, 128)
        pl.semaphore_signal(barrier, inc=1, device_id={"ev": lax.div(other, 16), "mesh": lax.rem(other, 16)},
                            device_id_type=MESH_ID)
        return carry

    lax.fori_loop(1, 128, greet, 0)

    fill_tables(ext, table, False)
    load.wait()
    for v in range(V):
        @pl.loop(0, E // 16)
        def _(b):
            e0 = pl.multiple_of(b * 16, 16)
            for c in range(C):
                xs[pl.ds((v * E + e0) * C + c, 16, stride=C), :] = kern[v, c, pl.ds(e0, 16), :].astype(jnp.float32)

    @pl.loop(0, TILES // FWD_UNROLL)
    def _(g):
        t0 = g * FWD_UNROLL
        for u in range(FWD_UNROLL):
            w = code_s[t0 + u]
            x = xs[pl.ds(((w >> 7) & 511) * C, 16), :].astype(jnp.bfloat16)
            scr[u * 16:u * 16 + 16, :] = jnp.dot(x, table[w & 127], preferred_element_type=jnp.float32)
        for h in range(FWD_UNROLL // 16):
            r0 = pl.multiple_of(t0 + h * 16, 16)
            for c in range(C):
                con[pl.ds(r0, 16), c * N:(c + 1) * N] = scr[pl.ds(h * 256 + c, 16, stride=16), :].astype(jnp.bfloat16)

    ids = lax.broadcasted_iota(jnp.int32, (128, N), 0)
    i_of, j_of, sub = ids >> 5, (ids >> 3) & 3, ids & 7
    block = code_ref[...] >> 16
    pl.semaphore_wait(barrier, 127)

    def partial(k, r):
        a1, a2, a3 = AXES[k]
        rows_k = i_of * WEIGHT[a2] + j_of * WEIGHT[a3] + sub
        halves = []
        for core_offset in (8, 0):
            wanted = block - (r * WEIGHT[a1] + core_offset)
            halves.append(jnp.concatenate([(rows_k == wanted[:, l * N:(l + 1) * N]).astype(jnp.float32).astype(jnp.bfloat16) for l in range(8)], axis=1))
        total = jnp.dot(jnp.concatenate(halves, axis=0), con[:, k * 512:(k + 1) * 512], preferred_element_type=jnp.float32)
        for cc in range(4):
            give[k, r, :, cc * 8:cc * 8 + 8, :] = total[:128, cc * N:(cc + 1) * N].reshape(16, 8, N)
        send(give.at[k, r], take.at[k, r], g_s, g_r.at[k, r], partner)
        for cc in range(4):
            own[k, r, :, cc * 8:cc * 8 + 8, :] = total[128:, cc * N:(cc + 1) * N].reshape(16, 8, N)

    def chip_sum(k, r):
        got(take.at[k, r], g_s, g_r.at[k, r])
        own[k, r] = own[k, r] + take[k, r]
        up, down = place(k, 1, 0, 0), place(k, 3, 0, 0)
        if r == 2:
            send(own.at[k, 2, pl.ds(0, 8)], s1.at[k, 0], s1_s, s1_r.at[k, 0], up)
            send(own.at[k, 2, pl.ds(8, 8)], s1.at[k, 1], s1_s, s1_r.at[k, 1], down)
        if r == 1:
            send(own.at[k, 1, pl.ds(8, 8)], s2.at[k, 0, pl.ds(8, 8)], s2_s, s2_r.at[k, 0, 1], up)
        if r == 3:
            send(own.at[k, 3, pl.ds(0, 8)], s2.at[k, 1, pl.ds(0, 8)], s2_s, s2_r.at[k, 1, 0], down)

    steps = [(k, r) for r in (2, 1, 3, 0) for k in range(3)]
    lag = 2
    for n, (k, r) in enumerate(steps):
        partial(k, r)
        if n >= lag:
            chip_sum(*steps[n - lag])
    for k, r in steps[len(steps) - lag:]:
        chip_sum(k, r)
    for k in range(3):
        got(s1.at[k, 0], s1_s, s1_r.at[k, 0])
        own[k, 1, 0:8] = own[k, 1, 0:8] + s1[k, 0]
        send(own.at[k, 1, pl.ds(0, 8)], s2.at[k, 0, pl.ds(0, 8)], s2_s, s2_r.at[k, 0, 0], place(k, 1, 0, 0))
        got(s1.at[k, 1], s1_s, s1_r.at[k, 1])
        own[k, 3, 8:16] = own[k, 3, 8:16] + s1[k, 1]
        send(own.at[k, 3, pl.ds(8, 8)], s2.at[k, 1, pl.ds(8, 8)], s2_s, s2_r.at[k, 1, 1], place(k, 3, 0, 0))
    far_first = sorted(range(1, 16), key=lambda q: -(HOPS[q // 4] + HOPS[q % 4]))
    for k in range(3):
        for way in range(2):
            for half in range(2):
                got(s2.at[k, way, pl.ds(half * 8, 8)], s2_s, s2_r.at[k, way, half])
        own[k, 0] = own[k, 0] + s2[k, 0] + s2[k, 1]
        for q in far_first:
            send(own.at[k, 0, q], pr.at[k, q - 1], p_s, p_r.at[k], place(k, 0, q // 4, q % 4))
    parts = []
    for k in range(3):
        got(pr.at[k], p_s, p_r.at[k])
        total = own[k, 0, 0]
        for q in range(15):
            total = total + pr[k, q]
        parts.append(total)
    gradient = jnp.concatenate(parts, axis=0)
    for one in loads:
        one.wait()
    prev_g, step, cond = (fields[n].reshape(96, N) for n in range(3))
    change = gradient - prev_g
    weighted = cond * change
    lane = lax.broadcasted_iota(jnp.int32, (1, N), 1)

    def summed(v):
        v = jnp.sum(v.reshape(12, 8, N), axis=0)
        return jnp.sum(jnp.sum(v, axis=0, keepdims=True), axis=1, keepdims=True)

    mine = jnp.zeros((1, N), jnp.float32)
    for n, v in enumerate((step * change, step * gradient, weighted * gradient, weighted * change)):
        mine = jnp.where(lane == n, summed(v), mine)
    row[...] = mine
    rows[me] = mine
    everyone = [(dx, dy, dz, other) for dx in range(4) for dy in range(4) for dz in range(4) for other in (False, True)][1:]
    for dx, dy, dz, other in sorted(everyone, key=lambda o: -(HOPS[o[0]] + HOPS[o[1]] + HOPS[o[2]])):
        send(row, rows.at[me], r_s, r_r, device(dx, dy, dz, other))
    got(rows.at[pl.ds(0, 127)], r_s, r_r)
    totals = jnp.sum(rows[...], axis=0)
    curvature, slope, cross, self_ = (
        jnp.sum(jnp.where(lane == n, totals, 0.0), axis=1, keepdims=True) for n in range(4))
    alpha = slope / curvature
    beta = (cross - alpha * self_) / curvature
    scaled = cond * (gradient - alpha * change)
    direction = -(scaled + (alpha - beta) * step)
    rounded = direction.astype(jnp.bfloat16)
    for k in range(3):
        tab[k, 0, 0, 0] = rounded[k * 32:(k + 1) * 32]
    for q in far_first:
        i, j = q // 4, q % 4
        back = (-i % 4) * 4 + (-j % 4)
        for k in range(3):
            send(tab.at[k, 0, 0, 0], tab.at[k, 0, 0, back], ap_s, ap_r.at[k, back // 4], place(k, 0, i, j))
    dir_ref[...] = direction.reshape(12, 1, 8, N)
    out_ref[TILES * C:, :] = jnp.zeros((16, N), jnp.float32)

    def spread(k, rc, r, i):
        a1, a2, a3 = AXES[k]
        for j in range(4):
            base = r * WEIGHT[a1] + i * WEIGHT[a2] + j * WEIGHT[a3] + rc * 8
            piece = tab[k, rc, r, i * 4 + j].astype(jnp.float32)
            for cc in range(4):
                out_ref[pl.ds(base * C + k * 4 + cc, 8, stride=C), :] = piece[cc * 8:cc * 8 + 8]

    def across(k, r, i):
        g = pl.ds(i * 4, 4)
        send(tab.at[k, 0, r, g], tab.at[k, 1, r, g], ad_s, ad_r.at[k, r, i], partner)

    for i in (0, 1, 3, 2):
        g = pl.ds(i * 4, 4)
        for k in range(3):
            got(tab.at[k, 0, 0, pl.ds(1, 3) if i == 0 else g], ap_s, ap_r.at[k, i])
            send(tab.at[k, 0, 0, g], tab.at[k, 0, 3, g], ar_s, ar_r.at[k, i, 0], place(k, 1, 0, 0))
            send(tab.at[k, 0, 0, g], tab.at[k, 0, 1, g], ar_s, ar_r.at[k, i, 1], place(k, 3, 0, 0))
            across(k, 0, i)
            spread(k, 0, 0, i)
    for i in (0, 1, 3, 2):
        g = pl.ds(i * 4, 4)
        for k in range(3):
            for way, r in ((0, 3), (1, 1)):
                got(tab.at[k, 0, r, g], ar_s, ar_r.at[k, i, way])
                if (way == 0) == (i < 2):
                    send(tab.at[k, 0, r, g], tab.at[k, 0, 2, g], a2_s, a2_r.at[k, i], place(k, 1 if way == 0 else 3, 0, 0))
                across(k, r, i)
                spread(k, 0, r, i)
    for i in (0, 1, 3, 2):
        for k in range(3):
            got(tab.at[k, 1, 0, pl.ds(i * 4, 4)], ad_s, ad_r.at[k, 0, i])
            spread(k, 1, 0, i)
    for i in (0, 1, 3, 2):
        for k in range(3):
            got(tab.at[k, 0, 2, pl.ds(i * 4, 4)], a2_s, a2_r.at[k, i])
            across(k, 2, i)
            spread(k, 0, 2, i)
    for r in (3, 1, 2):
        for i in (0, 1, 3, 2):
            for k in range(3):
                got(tab.at[k, 1, r, pl.ds(i * 4, 4)], ad_s, ad_r.at[k, r, i])
                spread(k, 1, r, i)
    sent(give, g_s, g_r.at[0, 0])
    sent(s1, s1_s, s1_r.at[0, 0])
    sent(s2, s2_s, s2_r.at[0, 0, 0])
    sent(pr, p_s, p_r.at[0])
    sent(rows.at[pl.ds(0, 127)], r_s, r_r)
    sent(tab.at[:, 0, 0, pl.ds(1, 15)], ap_s, ap_r.at[0, 0])
    sent(tab.at[:, 0, pl.ds(0, 2)], ar_s, ar_r.at[0, 0, 0])
    sent(tab.at[:, 0, 2], a2_s, a2_r.at[0, 0])
    sent(tab.at[:, 0], ad_s, ad_r.at[0, 0, 0])


def main(flat, code, kernels, prev_gradient, prev_step, precond):
    dma = pltpu.SemaphoreType.DMA
    f32, bf16 = jnp.float32, jnp.bfloat16
    vmem = pl.BlockSpec(memory_space=pltpu.VMEM)
    return pl.pallas_call(
        main_kernel,
        out_shape=(jax.ShapeDtypeStruct((C, 1, 8, N), f32), jax.ShapeDtypeStruct((TILES * C + 16, N), f32)),
        grid_spec=pltpu.PrefetchScalarGridSpec(
            num_scalar_prefetch=1, grid=(),
            in_specs=[vmem] + [pl.BlockSpec(memory_space=pltpu.HBM)] * 4,
            out_specs=(vmem, vmem),
            scratch_shapes=[
                pltpu.VMEM((V, C, E, N), bf16), pltpu.VMEM((3, C, 1, 8, N), f32), pltpu.VMEM((12, 136, N), f32), pltpu.VMEM((S, N, N), bf16),
                pltpu.VMEM((V * E * C + 16, N), f32), pltpu.VMEM((FWD_UNROLL * 16, N), f32), pltpu.VMEM((TILES, C * N), bf16),
                pltpu.VMEM((3, 4, 16, 32, N), f32), pltpu.VMEM((3, 4, 16, 32, N), f32), pltpu.VMEM((3, 4, 16, 32, N), f32),
                pltpu.VMEM((3, 2, 8, 32, N), f32), pltpu.VMEM((3, 2, 16, 32, N), f32), pltpu.VMEM((3, 15, 32, N), f32),
                pltpu.VMEM((1, N), f32), pltpu.VMEM((128, 1, N), f32), pltpu.VMEM((3, 2, 4, 16, 32, N), bf16),
            ] + [dma, dma((3,))] + [dma] * 9 + [dma((3, 4)), dma((3, 2)), dma((3, 2, 2)), dma((3,)), dma, dma((3, 4)), dma((3, 4, 2)), dma((3, 4)), dma((3, 4, 4))]),
        compiler_params=pltpu.CompilerParams(vmem_limit_bytes=44 << 20, collective_id=0, has_side_effects=True),
        name="main",
    )(flat, code, kernels, prev_gradient, prev_step, precond)


def bwd_kernel(code, xs, out_ref, ext, table, acc0, acc1):
    fill_tables(ext, table, True)
    zero = jnp.zeros((64, N), jnp.float32)

    @pl.loop(0, (E * C) // 64)
    def _(b):
        acc0[pl.ds(pl.multiple_of(b * 64, 64), 64), :] = zero
        acc1[pl.ds(pl.multiple_of(b * 64, 64), 64), :] = zero

    @pl.loop(0, T // BWD_UNROLL)
    def _(g):
        for u in range(BWD_UNROLL):
            for v, acc in ((0, acc0), (1, acc1)):
                w = code[v * T + g * BWD_UNROLL + u]
                block = w >> 16
                live = block < TILES
                x = xs[pl.ds(jnp.where(live, block, 0) * C, 16), :].astype(jnp.bfloat16)
                y = jnp.dot(x, table[w & 127], preferred_element_type=jnp.float32)
                r = jnp.where(live, (w >> 7) & 255, E) * C
                acc[pl.ds(r, 8), :] += y[:8]
                acc[pl.ds(r + 8, 4), :] += y[8:12]

    for v, acc in ((0, acc0), (1, acc1)):
        @pl.loop(0, E // 8)
        def _(b):
            e0 = pl.multiple_of(b * 8, 8)
            for c in range(C):
                out_ref[v, c, pl.ds(e0, 8), :] = acc[pl.ds(e0 * C + c, 8, stride=C), :]


def backward(code, dirs):
    f32 = jnp.float32
    return pl.pallas_call(
        bwd_kernel,
        out_shape=jax.ShapeDtypeStruct((V, C, E, N), f32),
        grid_spec=pltpu.PrefetchScalarGridSpec(
            num_scalar_prefetch=1, grid=(),
            in_specs=[pl.BlockSpec(memory_space=pltpu.VMEM)],
            out_specs=pl.BlockSpec(memory_space=pltpu.VMEM),
            scratch_shapes=[pltpu.VMEM((12, 136, N), f32), pltpu.VMEM((S, N, N), jnp.bfloat16),
                            pltpu.VMEM((E * C + 16, N), f32), pltpu.VMEM((E * C + 16, N), f32)]),
        compiler_params=pltpu.CompilerParams(vmem_limit_bytes=44 << 20),
        name="bwd",
    )(code, dirs)


def body(kernels, tile_owner, tile_source, tile_target, tile_seed, tile_count, prev_gradient, prev_step, precond):
    live = lax.broadcasted_iota(jnp.int32, (V, T), 1) < tile_count
    m = lax.axis_index("mesh")
    e = lax.axis_index("ev")
    owner = tile_owner.reshape(V, T)
    x = ((owner & 3) - (m & 3)) & 3
    y = ((owner >> 2) - (m >> 2)) & 3
    z = ((tile_target >> 4) - (e >> 1)) & 3
    c = ((tile_target >> 3) ^ e) & 1
    block = jnp.where(live, x * 256 + y * 64 + z * 16 + c * 8 + (tile_target & 7), TILES)
    src = tile_source + E * lax.broadcasted_iota(jnp.int32, (V, T), 0)
    code = tile_seed + (src << 7) + (block << 16)
    flat = code.reshape(TILES)
    direction, dirs = main(flat, code.reshape(1, TILES), kernels, prev_gradient, prev_step, precond)
    return direction, backward(flat, dirs)


def solution(mesh):
    in_specs = (
        P("ev", None, "mesh", None),
        P("ev", "mesh", None),
        P("ev", "mesh"),
        P("ev", "mesh"),
        P("ev", "mesh"),
        P("ev", "mesh"),
        P(None, "mesh", "ev", None),
        P(None, "mesh", "ev", None),
        P(None, "mesh", "ev", None),
    )
    out_specs = (P(None, "mesh", "ev", None), P("ev", None, "mesh", None))
    return jax.shard_map(body, mesh=mesh, in_specs=in_specs, out_specs=out_specs, check_vma=False)
```

time: 415 us -> 86.4 us (0.21)
  waiting for transfers between devices: 277 us -> 0 us
  blocking collectives: 64.6 us -> 0 us
  Pallas kernels: 38.9 us -> 80 us
  between operations: 17.4 us -> 0.67 us
  other arithmetic: 6.38 us -> 0.82 us
  matrix products: 5.35 us -> 0 us
    reduce_scatter x1 -> x0, waiting for transfers between devices: 215 us -> none  [body(): lax.psum_scatter(partial, ('mesh', 'ev'), scatter_dimension=0, tiled=True)]
    psum x1 -> x0, blocking collectives: 64.6 us -> none  [body(): curvature, slope, cross_term, self_term = lax.psum(sums, ('mesh', 'ev'))]
    all_gather x1 -> x0, waiting for transfers between devices: 62.8 us -> none  [body(): dirs = lax.all_gather(local, ('mesh', 'ev'), axis=0, tiled=True)]
    pallas_call x2, Pallas kernels: 38.9 us -> 80 us  [the longest x1 66.9 us: main(): pl.pallas_call(main_kernel, out_shape=(jax.ShapeDtypeStruct((C, 1, 8, N),...]
    dot_general x1 -> x0, matrix products: 5.35 us -> none  [body(): partial = jnp.dot(hits, contribution, preferred_element_type=jnp.float32)]
  transfers between devices with their start and end apart: 2 -> 0, of which waited for: 2 -> 0; matrix products, arithmetic and copies ran while one was open for 0% -> 0% of each run, Pallas kernels for 0% -> 0%
where the time goes in v3:
time: 86.4 us; the launch traced here: 85.9 us
  Pallas kernels  80 us (93%)
  local copies, waits for them, and re-layouts  4.42 us (5%)
    pallas_call x1, Pallas kernels, main(): pl.pallas_call(main_kernel, out_shape=(jax.ShapeDtypeStruct((C, 1, 8, N),...  66.9 us
    pallas_call x1, Pallas kernels, backward(): pl.pallas_call(bwd_kernel, out_shape=jax.ShapeDtypeStruct((V, C, E, N), f...  13.1 us
    unnamed x11, local copies, waits for them, and re-layouts  4.42 us

profile of v3, /device:TPU:1, one launch (start us, length us, event | category | flops | bytes accessed | tf_op | source)
XLA Modules:
  0.0 85.9 jit_solution(13840697703838477264)
XLA Ops:
  0.6 0.8 fusion.1
  1.5 0.0 copy-start
  1.5 1.4 %copy-done = bf16[2,12,256,128]{3,2,1,0:T(8,128)(2,1)S(1)} copy-done((bf16[2,12,256,128]{3,2,1,0:T(8,128)(2,1)S(1)}, bf16[2,12,256,128]{3,2,1,0:T(8,128)(2,1)}, u32[]{:S(2)}) %copy-start) | copy-done | bytes 1572888
  2.9 0.0 copy-start.1
  2.9 0.8 copy-done.1
  3.7 0.0 copy-start.2
  3.7 0.8 copy-done.2
  4.5 0.0 copy-start.3
  4.5 0.8 copy-done.3
  5.3 66.9 %main.1 = (f32[12,1,8,128]{3,2,1,0:T(8,128)S(1)}, f32[12304,128]{1,0:T(8,128)S(1)}) custom-call(s32[1024]{0:T(1024)S(1)} %bitcast.14, s32[1,1024]{1,0:T(1,128)S(1)} %bitcast.16, bf16[2,12,256,128]{3,2,1,0:T(8,128)(2,1)S(1)} %copy-done, f32[12,1,8,128]{3,2,1,0:T(8,128)S(1)} %copy-done.1, f32[12,1,8,128]{3,2,1,0:T(8,128)S(1)} %copy-done.2, ...), custom_call_target="tpu_custom_call" | custom-call | tf_op jit(solution)/shard_map/main/pallas_call | solution.py:264
  72.2 13.1 %bwd.1 = f32[2,12,256,128]{3,2,1,0:T(8,128)} custom-call(s32[1024]{0:T(1024)S(1)} %bitcast.15, f32[12304,128]{1,0:T(8,128)S(1)} %get-tuple-element.5.xs), custom_call_target="tpu_custom_call" | custom-call | tf_op jit(solution)/shard_map/bwd/pallas_call | solution.py:315
  85.3 0.6 copy.17
  (3 shorter events, 0.0 us)
Async XLA Ops:
  1.5 1.4 %copy-start = (bf16[2,12,256,128]{3,2,1,0:T(8,128)(2,1)S(1)}, bf16[2,12,256,128]{3,2,1,0:T(8,128)(2,1)}, u32[]{:S(2)}) copy-start(bf16[2,12,256,128]{3,2,1,0:T(8,128)(2,1)} %kern_hbm.1) | copy-start | bytes 4718596
  2.9 0.8 copy-start.1
  3.7 0.8 copy-start.2
  4.5 0.8 copy-start.3

commit v4 on v3

--- a/solution.py
+++ b/solution.py
@@ -11,8 +11,8 @@
 WEIGHT = (256, 64, 16)
 HOPS = (0, 1, 2, 1)
 MESH_ID = pl.DeviceIdType.MESH
-FWD_UNROLL = 64
-BWD_UNROLL = 64
+FWD_UNROLL = 128
+BWD_UNROLL = 128
 
 
 def fill_tables(ext, table, flip):
@@ -34,7 +34,7 @@
 def main_kernel(code_s, code_ref, kern_hbm, pg_hbm, ps_hbm, pc_hbm, dir_ref, out_ref,
                 kern, fields, ext, table, xs, scr, con, give, take, own, s1, s2, pr, row, rows, tab,
                 kern_sem, field_sem, g_s, s1_s, s2_s, p_s, r_s, ap_s, ar_s, a2_s, ad_s,
-                g_r, s1_r, s2_r, p_r, r_r, ap_r, ar_r, a2_r, ad_r):
+                g_r, s1_r, s2_r, d2_r, p_r, r_r, ap_r, ar_r, a2_r, ad_r):
     e = lax.axis_index("ev")
     m = lax.axis_index("mesh")
     me = e * 16 + m
@@ -42,9 +42,11 @@
     core = lax.rem(e, 2)
     coord = [[a if o == 0 else lax.rem(a + o, 4) for o in range(4)] for a in at]
 
+    ev_of = [(z * 2 + core, z * 2 + (1 - core)) for z in coord[2]]
+    mesh_of = [[y * 4 + x for x in coord[0]] for y in coord[1]]
+
     def device(dx, dy, dz, other=False):
-        c = 1 - core if other else core
-        return {"ev": coord[2][dz] * 2 + c, "mesh": coord[1][dy] * 4 + coord[0][dx]}
+        return {"ev": ev_of[dz][int(other)], "mesh": mesh_of[dy][dx]}
 
     def place(k, r, i, j):
         off = [0, 0, 0]
@@ -74,13 +76,10 @@
         one.start()
     barrier = pltpu.get_barrier_semaphore()
 
-    def greet(d, carry):
-        other = lax.rem(me + d, 128)
-        pl.semaphore_signal(barrier, inc=1, device_id={"ev": lax.div(other, 16), "mesh": lax.rem(other, 16)},
-                            device_id_type=MESH_ID)
-        return carry
-
-    lax.fori_loop(1, 128, greet, 0)
+    everyone = [(dx, dy, dz, other) for dx in range(4) for dy in range(4) for dz in range(4) for other in (False, True)][1:]
+    everyone.sort(key=lambda o: -(HOPS[o[0]] + HOPS[o[1]] + HOPS[o[2]]))
+    for dx, dy, dz, other in everyone:
+        pl.semaphore_signal(barrier, inc=1, device_id=device(dx, dy, dz, other), device_id_type=MESH_ID)
 
     fill_tables(ext, table, False)
     load.wait()
@@ -127,12 +126,12 @@
         own[k, r] = own[k, r] + take[k, r]
         up, down = place(k, 1, 0, 0), place(k, 3, 0, 0)
         if r == 2:
-            send(own.at[k, 2, pl.ds(0, 8)], s1.at[k, 0], s1_s, s1_r.at[k, 0], up)
-            send(own.at[k, 2, pl.ds(8, 8)], s1.at[k, 1], s1_s, s1_r.at[k, 1], down)
+            for i in (1, 2, 0, 3):
+                send(own.at[k, 2, pl.ds(i * 4, 4)], s1.at[k, i], s1_s, s1_r.at[k, i], up if i < 2 else down)
         if r == 1:
-            send(own.at[k, 1, pl.ds(8, 8)], s2.at[k, 0, pl.ds(8, 8)], s2_s, s2_r.at[k, 0, 1], up)
+            send(own.at[k, 1, pl.ds(8, 8)], s2.at[k, 0, pl.ds(8, 8)], s2_s, d2_r.at[k, 0], up)
         if r == 3:
-            send(own.at[k, 3, pl.ds(0, 8)], s2.at[k, 1, pl.ds(0, 8)], s2_s, s2_r.at[k, 1, 0], down)
+            send(own.at[k, 3, pl.ds(0, 8)], s2.at[k, 1, pl.ds(0, 8)], s2_s, d2_r.at[k, 1], down)
 
     steps = [(k, r) for r in (2, 1, 3, 0) for k in range(3)]
     lag = 2
@@ -142,21 +141,25 @@
             chip_sum(*steps[n - lag])
     for k, r in steps[len(steps) - lag:]:
         chip_sum(k, r)
-    for k in range(3):
-        got(s1.at[k, 0], s1_s, s1_r.at[k, 0])
-        own[k, 1, 0:8] = own[k, 1, 0:8] + s1[k, 0]
-        send(own.at[k, 1, pl.ds(0, 8)], s2.at[k, 0, pl.ds(0, 8)], s2_s, s2_r.at[k, 0, 0], place(k, 1, 0, 0))
-        got(s1.at[k, 1], s1_s, s1_r.at[k, 1])
-        own[k, 3, 8:16] = own[k, 3, 8:16] + s1[k, 1]
-        send(own.at[k, 3, pl.ds(8, 8)], s2.at[k, 1, pl.ds(8, 8)], s2_s, s2_r.at[k, 1, 1], place(k, 3, 0, 0))
+    for i in (1, 2, 0, 3):
+        g = pl.ds(i * 4, 4)
+        for k in range(3):
+            r, way = (1, 0) if i < 2 else (3, 1)
+            got(s1.at[k, i], s1_s, s1_r.at[k, i])
+            own[k, r, g] = own[k, r, g] + s1[k, i]
+            send(own.at[k, r, g], s2.at[k, way, g], s2_s, s2_r.at[k, i], place(k, r, 0, 0))
     far_first = sorted(range(1, 16), key=lambda q: -(HOPS[q // 4] + HOPS[q % 4]))
-    for k in range(3):
-        for way in range(2):
-            for half in range(2):
-                got(s2.at[k, way, pl.ds(half * 8, 8)], s2_s, s2_r.at[k, way, half])
-        own[k, 0] = own[k, 0] + s2[k, 0] + s2[k, 1]
-        for q in far_first:
-            send(own.at[k, 0, q], pr.at[k, q - 1], p_s, p_r.at[k], place(k, 0, q // 4, q % 4))
+    for i in (1, 2, 0, 3):
+        g = pl.ds(i * 4, 4)
+        for k in range(3):
+            if i == 1:
+                got(s2.at[k, 0, pl.ds(8, 8)], s2_s, d2_r.at[k, 0])
+                got(s2.at[k, 1, pl.ds(0, 8)], s2_s, d2_r.at[k, 1])
+            got(s2.at[k, 0 if i < 2 else 1, g], s2_s, s2_r.at[k, i])
+            own[k, 0, g] = own[k, 0, g] + s2[k, 0, g] + s2[k, 1, g]
+            for q in far_first:
+                if q // 4 == i:
+                    send(own.at[k, 0, q], pr.at[k, q - 1], p_s, p_r.at[k], place(k, 0, i, q % 4))
     parts = []
     for k in range(3):
         got(pr.at[k], p_s, p_r.at[k])
@@ -181,8 +184,7 @@
         mine = jnp.where(lane == n, summed(v), mine)
     row[...] = mine
     rows[me] = mine
-    everyone = [(dx, dy, dz, other) for dx in range(4) for dy in range(4) for dz in range(4) for other in (False, True)][1:]
-    for dx, dy, dz, other in sorted(everyone, key=lambda o: -(HOPS[o[0]] + HOPS[o[1]] + HOPS[o[2]])):
+    for dx, dy, dz, other in everyone:
         send(row, rows.at[me], r_s, r_r, device(dx, dy, dz, other))
     got(rows.at[pl.ds(0, 127)], r_s, r_r)
     totals = jnp.sum(rows[...], axis=0)
@@ -221,6 +223,8 @@
             got(tab.at[k, 0, 0, pl.ds(1, 3) if i == 0 else g], ap_s, ap_r.at[k, i])
             send(tab.at[k, 0, 0, g], tab.at[k, 0, 3, g], ar_s, ar_r.at[k, i, 0], place(k, 1, 0, 0))
             send(tab.at[k, 0, 0, g], tab.at[k, 0, 1, g], ar_s, ar_r.at[k, i, 1], place(k, 3, 0, 0))
+            if i == 2:
+                send(tab.at[k, 0, 0, g], tab.at[k, 0, 2, g], a2_s, a2_r.at[k, i], place(k, 2, 0, 0))
             across(k, 0, i)
             spread(k, 0, 0, i)
     for i in (0, 1, 3, 2):
@@ -228,7 +232,7 @@
         for k in range(3):
             for way, r in ((0, 3), (1, 1)):
                 got(tab.at[k, 0, r, g], ar_s, ar_r.at[k, i, way])
-                if (way == 0) == (i < 2):
+                if i != 2 and (way == 0) == (i < 2):
                     send(tab.at[k, 0, r, g], tab.at[k, 0, 2, g], a2_s, a2_r.at[k, i], place(k, 1 if way == 0 else 3, 0, 0))
                 across(k, r, i)
                 spread(k, 0, r, i)
@@ -248,7 +252,7 @@
                 spread(k, 1, r, i)
     sent(give, g_s, g_r.at[0, 0])
     sent(s1, s1_s, s1_r.at[0, 0])
-    sent(s2, s2_s, s2_r.at[0, 0, 0])
+    sent(s2, s2_s, s2_r.at[0, 0])
     sent(pr, p_s, p_r.at[0])
     sent(rows.at[pl.ds(0, 127)], r_s, r_r)
     sent(tab.at[:, 0, 0, pl.ds(1, 15)], ap_s, ap_r.at[0, 0])
@@ -272,15 +276,15 @@
                 pltpu.VMEM((V, C, E, N), bf16), pltpu.VMEM((3, C, 1, 8, N), f32), pltpu.VMEM((12, 136, N), f32), pltpu.VMEM((S, N, N), bf16),
                 pltpu.VMEM((V * E * C + 16, N), f32), pltpu.VMEM((FWD_UNROLL * 16, N), f32), pltpu.VMEM((TILES, C * N), bf16),
                 pltpu.VMEM((3, 4, 16, 32, N), f32), pltpu.VMEM((3, 4, 16, 32, N), f32), pltpu.VMEM((3, 4, 16, 32, N), f32),
-                pltpu.VMEM((3, 2, 8, 32, N), f32), pltpu.VMEM((3, 2, 16, 32, N), f32), pltpu.VMEM((3, 15, 32, N), f32),
+                pltpu.VMEM((3, 4, 4, 32, N), f32), pltpu.VMEM((3, 2, 16, 32, N), f32), pltpu.VMEM((3, 15, 32, N), f32),
                 pltpu.VMEM((1, N), f32), pltpu.VMEM((128, 1, N), f32), pltpu.VMEM((3, 2, 4, 16, 32, N), bf16),
-            ] + [dma, dma((3,))] + [dma] * 9 + [dma((3, 4)), dma((3, 2)), dma((3, 2, 2)), dma((3,)), dma, dma((3, 4)), dma((3, 4, 2)), dma((3, 4)), dma((3, 4, 4))]),
+            ] + [dma, dma((3,))] + [dma] * 9 + [dma((3, 4)), dma((3, 4)), dma((3, 4)), dma((3, 2)), dma((3,)), dma, dma((3, 4)), dma((3, 4, 2)), dma((3, 4)), dma((3, 4, 4))]),
         compiler_params=pltpu.CompilerParams(vmem_limit_bytes=44 << 20, collective_id=0, has_side_effects=True),
         name="main",
-    )(flat, code, kernels, prev_gradient, prev_step, precond)
-
-
-def bwd_kernel(code, xs, out_ref, ext, table, acc0, acc1):
+    )(flat, code, *(pltpu.with_memory_space_constraint(v, pltpu.HBM) for v in (kernels, prev_gradient, prev_step, precond)))
+
+
+def bwd_kernel(code, xs, dir_ref, out_ref, dir_out, ext, table, acc0, acc1, stage, sem):
     fill_tables(ext, table, True)
     zero = jnp.zeros((64, N), jnp.float32)
 
@@ -302,28 +306,39 @@
                 acc[pl.ds(r, 8), :] += y[:8]
                 acc[pl.ds(r + 8, 4), :] += y[8:12]
 
-    for v, acc in ((0, acc0), (1, acc1)):
-        @pl.loop(0, E // 8)
+    def leave(n):
+        return pltpu.make_async_copy(stage.at[n], out_ref.at[n // 4, :, pl.ds(n % 4 * 64, 64)], sem.at[n])
+
+    for n in range(8):
+        acc = (acc0, acc1)[n // 4]
+
+        @pl.loop(0, 8)
         def _(b):
             e0 = pl.multiple_of(b * 8, 8)
             for c in range(C):
-                out_ref[v, c, pl.ds(e0, 8), :] = acc[pl.ds(e0 * C + c, 8, stride=C), :]
-
-
-def backward(code, dirs):
+                stage[n, c, pl.ds(e0, 8), :] = acc[pl.ds((n % 4 * 64 + e0) * C + c, 8, stride=C), :]
+
+        leave(n).start()
+    dir_out[...] = dir_ref[...]
+    for n in range(8):
+        leave(n).wait()
+
+
+def backward(code, dirs, direction):
     f32 = jnp.float32
     return pl.pallas_call(
         bwd_kernel,
-        out_shape=jax.ShapeDtypeStruct((V, C, E, N), f32),
+        out_shape=(jax.ShapeDtypeStruct((V, C, E, N), f32), jax.ShapeDtypeStruct((C, 1, 8, N), f32)),
         grid_spec=pltpu.PrefetchScalarGridSpec(
             num_scalar_prefetch=1, grid=(),
-            in_specs=[pl.BlockSpec(memory_space=pltpu.VMEM)],
-            out_specs=pl.BlockSpec(memory_space=pltpu.VMEM),
+            in_specs=[pl.BlockSpec(memory_space=pltpu.VMEM)] * 2,
+            out_specs=(pl.BlockSpec(memory_space=pl.ANY), pl.BlockSpec(memory_space=pltpu.VMEM)),
             scratch_shapes=[pltpu.VMEM((12, 136, N), f32), pltpu.VMEM((S, N, N), jnp.bfloat16),
-                            pltpu.VMEM((E * C + 16, N), f32), pltpu.VMEM((E * C + 16, N), f32)]),
+                            pltpu.VMEM((E * C + 16, N), f32), pltpu.VMEM((E * C + 16, N), f32),
+                            pltpu.VMEM((8, C, 64, N), f32), pltpu.SemaphoreType.DMA((8,))]),
         compiler_params=pltpu.CompilerParams(vmem_limit_bytes=44 << 20),
         name="bwd",
-    )(code, dirs)
+    )(code, dirs, direction)
 
 
 def body(kernels, tile_owner, tile_source, tile_target, tile_seed, tile_count, prev_gradient, prev_step, precond):
@@ -340,7 +355,8 @@
     code = tile_seed + (src << 7) + (block << 16)
     flat = code.reshape(TILES)
     direction, dirs = main(flat, code.reshape(1, TILES), kernels, prev_gradient, prev_step, precond)
-    return direction, backward(flat, dirs)
+    event_direction, direction = backward(flat, dirs, direction)
+    return direction, event_direction
 
 
 def solution(mesh):

time: 86.4 us -> 77.1 us (0.89)
  Pallas kernels: 80 us -> 75.3 us
  local copies, waits for them, and re-layouts: 4.42 us -> 0.01 us
    pallas_call x1, Pallas kernels: 66.9 us -> 62.4 us  [main(): pl.pallas_call(main_kernel, out_shape=(jax.ShapeDtypeStruct((C, 1, 8, N),...]
    unnamed x11 -> x2, local copies, waits for them, and re-layouts: 4.42 us -> 0.01 us
where the time goes in v4:
time: 77.1 us; the launch traced here: 76.8 us
  Pallas kernels  75.3 us (98%)
  other arithmetic  0.82 us (1%)
    pallas_call x1, Pallas kernels, main(): pl.pallas_call(main_kernel, out_shape=(jax.ShapeDtypeStruct((C, 1, 8, N),...  62.4 us
    pallas_call x1, Pallas kernels, backward(): pl.pallas_call(bwd_kernel, out_shape=(jax.ShapeDtypeStruct((V, C, E, N),...  12.9 us

profile of v4, /device:TPU:1, one launch (start us, length us, event | category | flops | bytes accessed | tf_op | source)
XLA Modules:
  0.0 76.8 jit_solution(1076177241584644813)
XLA Ops:
  0.6 0.8 %fusion.1 = s32[2,512]{1,0:T(2,128)S(1)} fusion(s32[2,512]{1,0:T(2,128)} %param.12, s32[2,512,1]{1,2,0:T(1,128)} %param.10, s32[2,512]{1,0:T(2,128)} %param.13, s32[2,512]{1,0:T(2,128)} %param.11, s32[2]{0:T(128)S(1)} %iota_multiply_fusion, s32[2]{0:T(128)} %bitcast.19, s32[]{:T(128)S(6)} %axis_index.25, s32[]{:T(128)S(6)} %shift_right_arithmetic.27, ...), kind=kLoop, calls=%fused_computation.2 | loop fusion | flops 28672 | bytes 20512 | tf_op jit(solution)/shard_map/add | solution.py:355
  1.5 62.4 %main.1 = (f32[12,1,8,128]{3,2,1,0:T(8,128)S(1)}, f32[12304,128]{1,0:T(8,128)S(1)}) custom-call(s32[1024]{0:T(1024)S(1)} %bitcast.14, s32[1,1024]{1,0:T(1,128)S(1)} %bitcast.16, bf16[2,12,256,128]{3,2,1,0:T(8,128)(2,1)} %kern_hbm.1, f32[12,1,8,128]{3,2,1,0:T(8,128)} %pg_hbm.1, f32[12,1,8,128]{3,2,1,0:T(8,128)} %ps_hbm.1, f32[12,1,8,128]{3,2,1,0:T(8,128)} %pc_hbm.1), custom_call_target="tpu_custom_call" | custom-call | tf_op jit(solution)/shard_map/main/pallas_call | solution.py:268
  63.8 12.9 %bwd.1 = (f32[2,12,256,128]{3,2,1,0:T(8,128)}, f32[12,1,8,128]{3,2,1,0:T(8,128)}) custom-call(s32[1024]{0:T(1024)S(1)} %bitcast.15, f32[12304,128]{1,0:T(8,128)S(1)} %get-tuple-element.6.xs, f32[12,1,8,128]{3,2,1,0:T(8,128)S(1)} %get-tuple-element.7.dir_ref), custom_call_target="tpu_custom_call" | custom-call | tf_op jit(solution)/shard_map/bwd/pallas_call | solution.py:329
  (3 shorter events, 0.0 us)

commit v5 on v4

--- a/solution.py
+++ b/solution.py
@@ -11,7 +11,7 @@
 WEIGHT = (256, 64, 16)
 HOPS = (0, 1, 2, 1)
 MESH_ID = pl.DeviceIdType.MESH
-FWD_UNROLL = 128
+FWD_UNROLL = 256
 BWD_UNROLL = 128
 
 
@@ -31,9 +31,9 @@
             table[k * 7 + o] = ext[k, pl.ds(4 - off, N), :].astype(jnp.bfloat16)
 
 
-def main_kernel(code_s, code_ref, kern_hbm, pg_hbm, ps_hbm, pc_hbm, dir_ref, out_ref,
-                kern, fields, ext, table, xs, scr, con, give, take, own, s1, s2, pr, row, rows, tab,
-                kern_sem, field_sem, g_s, s1_s, s2_s, p_s, r_s, ap_s, ar_s, a2_s, ad_s,
+def main_kernel(count_hbm, kern_hbm, owner_hbm, target_hbm, seed_hbm, source_hbm, pg_hbm, ps_hbm, pc_hbm, dir_ref, out_ref, code_ref,
+                seed_s, source_s, count, owner, words, kern, fields, ext, table, xs, scr, con, give, take, own, s1, s2, pr, row, rows, tab,
+                kern_sem, word_sem, field_sem, g_s, s1_s, s2_s, p_s, r_s, ap_s, ar_s, a2_s, ad_s,
                 g_r, s1_r, s2_r, d2_r, p_r, r_r, ap_r, ar_r, a2_r, ad_r):
     e = lax.axis_index("ev")
     m = lax.axis_index("mesh")
@@ -71,6 +71,10 @@
 
     load = pltpu.make_async_copy(kern_hbm, kern, kern_sem)
     load.start()
+    indices = [pltpu.make_async_copy(src, dst, word_sem.at[n]) for n, (src, dst) in enumerate((
+        (seed_hbm, seed_s), (source_hbm, source_s), (owner_hbm, owner), (target_hbm, words.at[0]), (seed_hbm, words.at[1]), (source_hbm, words.at[2]), (count_hbm, count)))]
+    for one in indices:
+        one.start()
     loads = [pltpu.make_async_copy(src, fields.at[n], field_sem.at[n]) for n, src in enumerate((pg_hbm, ps_hbm, pc_hbm))]
     for one in loads:
         one.start()
@@ -83,6 +87,20 @@
 
     fill_tables(ext, table, False)
     load.wait()
+    for one in indices:
+        one.wait()
+    lanes = lax.broadcasted_iota(jnp.int32, (1, T), 1)
+    blocks = []
+    for v in range(V):
+        home, goal = owner[v], words[0, v:v + 1, :]
+        dx = ((home & 3) - at[0]) & 3
+        dy = ((home >> 2) - at[1]) & 3
+        dz = ((goal >> 4) - at[2]) & 3
+        dc = ((goal >> 3) - core) & 1
+        block = dx * 256 + dy * 64 + dz * 16 + dc * 8 + (goal & 7)
+        block = jnp.where(lanes < count[0:1, v:v + 1], block, TILES)
+        code_ref[v:v + 1, :] = words[1, v:v + 1, :] + (words[2, v:v + 1, :] << 7) + (block << 16)
+        blocks.append(block)
     for v in range(V):
         @pl.loop(0, E // 16)
         def _(b):
@@ -94,9 +112,10 @@
     def _(g):
         t0 = g * FWD_UNROLL
         for u in range(FWD_UNROLL):
-            w = code_s[t0 + u]
-            x = xs[pl.ds(((w >> 7) & 511) * C, 16), :].astype(jnp.bfloat16)
-            scr[u * 16:u * 16 + 16, :] = jnp.dot(x, table[w & 127], preferred_element_type=jnp.float32)
+            t = (g % (T // FWD_UNROLL)) * FWD_UNROLL + u
+            v = g // (T // FWD_UNROLL)
+            x = xs[pl.ds((v * E + source_s[v, t]) * C, 16), :].astype(jnp.bfloat16)
+            scr[u * 16:u * 16 + 16, :] = jnp.dot(x, table[seed_s[v, t]], preferred_element_type=jnp.float32)
         for h in range(FWD_UNROLL // 16):
             r0 = pl.multiple_of(t0 + h * 16, 16)
             for c in range(C):
@@ -104,7 +123,7 @@
 
     ids = lax.broadcasted_iota(jnp.int32, (128, N), 0)
     i_of, j_of, sub = ids >> 5, (ids >> 3) & 3, ids & 7
-    block = code_ref[...] >> 16
+    block = jnp.concatenate(blocks, axis=1)
     pl.semaphore_wait(barrier, 127)
 
     def partial(k, r):
@@ -202,6 +221,7 @@
         back = (-i % 4) * 4 + (-j % 4)
         for k in range(3):
             send(tab.at[k, 0, 0, 0], tab.at[k, 0, 0, back], ap_s, ap_r.at[k, back // 4], place(k, 0, i, j))
+
     dir_ref[...] = direction.reshape(12, 1, 8, N)
     out_ref[TILES * C:, :] = jnp.zeros((16, N), jnp.float32)
 
@@ -221,31 +241,23 @@
         g = pl.ds(i * 4, 4)
         for k in range(3):
             got(tab.at[k, 0, 0, pl.ds(1, 3) if i == 0 else g], ap_s, ap_r.at[k, i])
+            send(tab.at[k, 0, 0, g], tab.at[k, 0, 2, g], a2_s, a2_r.at[k, i], place(k, 2, 0, 0))
             send(tab.at[k, 0, 0, g], tab.at[k, 0, 3, g], ar_s, ar_r.at[k, i, 0], place(k, 1, 0, 0))
             send(tab.at[k, 0, 0, g], tab.at[k, 0, 1, g], ar_s, ar_r.at[k, i, 1], place(k, 3, 0, 0))
-            if i == 2:
-                send(tab.at[k, 0, 0, g], tab.at[k, 0, 2, g], a2_s, a2_r.at[k, i], place(k, 2, 0, 0))
             across(k, 0, i)
             spread(k, 0, 0, i)
     for i in (0, 1, 3, 2):
         g = pl.ds(i * 4, 4)
-        for k in range(3):
-            for way, r in ((0, 3), (1, 1)):
-                got(tab.at[k, 0, r, g], ar_s, ar_r.at[k, i, way])
-                if i != 2 and (way == 0) == (i < 2):
-                    send(tab.at[k, 0, r, g], tab.at[k, 0, 2, g], a2_s, a2_r.at[k, i], place(k, 1 if way == 0 else 3, 0, 0))
+        for way, r in ((0, 3), (1, 1), (2, 2)):
+            for k in range(3):
+                got(tab.at[k, 0, r, g], ar_s, a2_r.at[k, i] if way == 2 else ar_r.at[k, i, way])
                 across(k, r, i)
-                spread(k, 0, r, i)
-    for i in (0, 1, 3, 2):
-        for k in range(3):
-            got(tab.at[k, 1, 0, pl.ds(i * 4, 4)], ad_s, ad_r.at[k, 0, i])
-            spread(k, 1, 0, i)
-    for i in (0, 1, 3, 2):
-        for k in range(3):
-            got(tab.at[k, 0, 2, pl.ds(i * 4, 4)], a2_s, a2_r.at[k, i])
-            across(k, 2, i)
-            spread(k, 0, 2, i)
-    for r in (3, 1, 2):
+    for r in (0, 3, 1, 2):
+        for i in (0, 1, 3, 2):
+            for k in range(3):
+                if r:
+                    spread(k, 0, r, i)
+    for r in (0, 3, 1, 2):
         for i in (0, 1, 3, 2):
             for k in range(3):
                 got(tab.at[k, 1, r, pl.ds(i * 4, 4)], ad_s, ad_r.at[k, r, i])
@@ -261,27 +273,28 @@
     sent(tab.at[:, 0], ad_s, ad_r.at[0, 0, 0])
 
 
-def main(flat, code, kernels, prev_gradient, prev_step, precond):
+def main(*arrays):
     dma = pltpu.SemaphoreType.DMA
-    f32, bf16 = jnp.float32, jnp.bfloat16
+    f32, bf16, i32 = jnp.float32, jnp.bfloat16, jnp.int32
     vmem = pl.BlockSpec(memory_space=pltpu.VMEM)
     return pl.pallas_call(
         main_kernel,
-        out_shape=(jax.ShapeDtypeStruct((C, 1, 8, N), f32), jax.ShapeDtypeStruct((TILES * C + 16, N), f32)),
+        out_shape=(jax.ShapeDtypeStruct((C, 1, 8, N), f32), jax.ShapeDtypeStruct((TILES * C + 16, N), f32), jax.ShapeDtypeStruct((V, T), i32)),
         grid_spec=pltpu.PrefetchScalarGridSpec(
-            num_scalar_prefetch=1, grid=(),
-            in_specs=[vmem] + [pl.BlockSpec(memory_space=pltpu.HBM)] * 4,
-            out_specs=(vmem, vmem),
+            num_scalar_prefetch=0, grid=(),
+            in_specs=[pl.BlockSpec(memory_space=pltpu.HBM)] * len(arrays),
+            out_specs=(vmem, vmem, vmem),
             scratch_shapes=[
+                pltpu.SMEM((V, T), i32), pltpu.SMEM((V, T), i32), pltpu.VMEM((1, V), i32), pltpu.VMEM((V, 1, T), i32), pltpu.VMEM((3, V, T), i32),
                 pltpu.VMEM((V, C, E, N), bf16), pltpu.VMEM((3, C, 1, 8, N), f32), pltpu.VMEM((12, 136, N), f32), pltpu.VMEM((S, N, N), bf16),
                 pltpu.VMEM((V * E * C + 16, N), f32), pltpu.VMEM((FWD_UNROLL * 16, N), f32), pltpu.VMEM((TILES, C * N), bf16),
                 pltpu.VMEM((3, 4, 16, 32, N), f32), pltpu.VMEM((3, 4, 16, 32, N), f32), pltpu.VMEM((3, 4, 16, 32, N), f32),
                 pltpu.VMEM((3, 4, 4, 32, N), f32), pltpu.VMEM((3, 2, 16, 32, N), f32), pltpu.VMEM((3, 15, 32, N), f32),
                 pltpu.VMEM((1, N), f32), pltpu.VMEM((128, 1, N), f32), pltpu.VMEM((3, 2, 4, 16, 32, N), bf16),
-            ] + [dma, dma((3,))] + [dma] * 9 + [dma((3, 4)), dma((3, 4)), dma((3, 4)), dma((3, 2)), dma((3,)), dma, dma((3, 4)), dma((3, 4, 2)), dma((3, 4)), dma((3, 4, 4))]),
+            ] + [dma, dma((7,)), dma((3,))] + [dma] * 9 + [dma((3, 4)), dma((3, 4)), dma((3, 4)), dma((3, 2)), dma((3,)), dma, dma((3, 4)), dma((3, 4, 2)), dma((3, 4)), dma((3, 4, 4))]),
         compiler_params=pltpu.CompilerParams(vmem_limit_bytes=44 << 20, collective_id=0, has_side_effects=True),
         name="main",
-    )(flat, code, *(pltpu.with_memory_space_constraint(v, pltpu.HBM) for v in (kernels, prev_gradient, prev_step, precond)))
+    )(*(pltpu.with_memory_space_constraint(v, pltpu.HBM) for v in arrays))
 
 
 def bwd_kernel(code, xs, dir_ref, out_ref, dir_out, ext, table, acc0, acc1, stage, sem):
@@ -297,7 +310,7 @@
     def _(g):
         for u in range(BWD_UNROLL):
             for v, acc in ((0, acc0), (1, acc1)):
-                w = code[v * T + g * BWD_UNROLL + u]
+                w = code[v, g * BWD_UNROLL + u]
                 block = w >> 16
                 live = block < TILES
                 x = xs[pl.ds(jnp.where(live, block, 0) * C, 16), :].astype(jnp.bfloat16)
@@ -342,20 +355,9 @@
 
 
 def body(kernels, tile_owner, tile_source, tile_target, tile_seed, tile_count, prev_gradient, prev_step, precond):
-    live = lax.broadcasted_iota(jnp.int32, (V, T), 1) < tile_count
-    m = lax.axis_index("mesh")
-    e = lax.axis_index("ev")
-    owner = tile_owner.reshape(V, T)
-    x = ((owner & 3) - (m & 3)) & 3
-    y = ((owner >> 2) - (m >> 2)) & 3
-    z = ((tile_target >> 4) - (e >> 1)) & 3
-    c = ((tile_target >> 3) ^ e) & 1
-    block = jnp.where(live, x * 256 + y * 64 + z * 16 + c * 8 + (tile_target & 7), TILES)
-    src = tile_source + E * lax.broadcasted_iota(jnp.int32, (V, T), 0)
-    code = tile_seed + (src << 7) + (block << 16)
-    flat = code.reshape(TILES)
-    direction, dirs = main(flat, code.reshape(1, TILES), kernels, prev_gradient, prev_step, precond)
-    event_direction, direction = backward(flat, dirs, direction)
+    direction, dirs, code = main(tile_count.reshape(1, V), kernels, tile_owner.reshape(V, 1, T), tile_target, tile_seed, tile_source,
+                                 prev_gradient, prev_step, precond)
+    event_direction, direction = backward(code, dirs, direction)
     return direction, event_direction
 
 

time: 77.1 us -> 74.4 us (0.965)
  Pallas kernels: 75.3 us -> 73.7 us
  other arithmetic: 0.82 us -> 0 us
    pallas_call x1, Pallas kernels: 62.4 us -> 60.6 us  [main(): pl.pallas_call(main_kernel, out_shape=(jax.ShapeDtypeStruct((C, 1, 8, N),...]
    add x1 -> x0, other arithmetic: 0.82 us -> none  [body(): code = tile_seed + (src << 7) + (block << 16)]
where the time goes in v5:
time: 74.4 us; the launch traced here: 74.3 us
  Pallas kernels  73.7 us (99%)
    pallas_call x1, Pallas kernels, main(): pl.pallas_call(main_kernel, out_shape=(jax.ShapeDtypeStruct((C, 1, 8, N),...  60.6 us
    pallas_call x1, Pallas kernels, backward(): pl.pallas_call(bwd_kernel, out_shape=(jax.ShapeDtypeStruct((V, C, E, N),...  13.1 us

profile of v5, /device:TPU:1, one launch (start us, length us, event | category | flops | bytes accessed | tf_op | source)
XLA Modules:
  0.0 74.3 jit_solution(2315880027314709812)
XLA Ops:
  0.6 60.6 %main.1 = (f32[12,1,8,128]{3,2,1,0:T(8,128)S(1)}, f32[12304,128]{1,0:T(8,128)S(1)}, s32[2,512]{1,0:T(2,128)S(1)}) custom-call(s32[1,2]{1,0:T(1,128)} %bitcast.3, bf16[2,12,256,128]{3,2,1,0:T(8,128)(2,1)} %kern_hbm.1, s32[2,1,512]{2,1,0:T(1,128)} %bitcast.2, s32[2,512]{1,0:T(2,128)} %target_hbm.1, s32[2,512]{1,0:T(2,128)} %seed_hbm.1, s32[2,512]{1,0:T(2,128)} %source_hbm.1, ...), custom_call_target="tpu_custom_call" | custom-call | tf_op jit(solution)/shard_map/main/pallas_call | solution.py:280
  61.2 13.1 %bwd.1 = (f32[2,12,256,128]{3,2,1,0:T(8,128)}, f32[12,1,8,128]{3,2,1,0:T(8,128)}) custom-call(s32[2,512]{1,0:T(2,128)S(1)} %get-tuple-element.7.code, f32[12304,128]{1,0:T(8,128)S(1)} %get-tuple-element.8.xs, f32[12,1,8,128]{3,2,1,0:T(8,128)S(1)} %get-tuple-element.9.dir_ref), custom_call_target="tpu_custom_call" | custom-call | tf_op jit(solution)/shard_map/bwd/pallas_call | solution.py:342

commit v6 on v5

--- a/solution.py
+++ b/solution.py
@@ -15,7 +15,7 @@
 BWD_UNROLL = 128
 
 
-def fill_tables(ext, table, flip):
+def fill_tables(ext, table):
     i = lax.broadcasted_iota(jnp.int32, (136, N), 0).astype(jnp.float32) - 4.0
     j = lax.broadcasted_iota(jnp.int32, (136, N), 1).astype(jnp.float32)
     d = i - j
@@ -27,12 +27,11 @@
             ext[wt * 3 + sp] = weight * e
     for k in range(12):
         for o in range(7):
-            off = 3 - o if flip else o - 3
-            table[k * 7 + o] = ext[k, pl.ds(4 - off, N), :].astype(jnp.bfloat16)
-
-
-def main_kernel(count_hbm, kern_hbm, owner_hbm, target_hbm, seed_hbm, source_hbm, pg_hbm, ps_hbm, pc_hbm, dir_ref, out_ref, code_ref,
-                seed_s, source_s, count, owner, words, kern, fields, ext, table, xs, scr, con, give, take, own, s1, s2, pr, row, rows, tab,
+            table[k * 7 + o] = ext[k, pl.ds(7 - o, N), :].astype(jnp.bfloat16)
+
+
+def main_kernel(count_hbm, kern_hbm, owner_hbm, target_hbm, seed_hbm, source_hbm, pg_hbm, ps_hbm, pc_hbm, dir_ref, out_ref, code_ref, table,
+                seed_s, source_s, count, owner, words, kern, fields, ext, xs, scr, con, give, take, own, s1, s2, pr, row, rows, tab,
                 kern_sem, word_sem, field_sem, g_s, s1_s, s2_s, p_s, r_s, ap_s, ar_s, a2_s, ad_s,
                 g_r, s1_r, s2_r, d2_r, p_r, r_r, ap_r, ar_r, a2_r, ad_r):
     e = lax.axis_index("ev")
@@ -85,7 +84,7 @@
     for dx, dy, dz, other in everyone:
         pl.semaphore_signal(barrier, inc=1, device_id=device(dx, dy, dz, other), device_id_type=MESH_ID)
 
-    fill_tables(ext, table, False)
+    fill_tables(ext, table)
     load.wait()
     for one in indices:
         one.wait()
@@ -99,7 +98,9 @@
         dc = ((goal >> 3) - core) & 1
         block = dx * 256 + dy * 64 + dz * 16 + dc * 8 + (goal & 7)
         block = jnp.where(lanes < count[0:1, v:v + 1], block, TILES)
-        code_ref[v:v + 1, :] = words[1, v:v + 1, :] + (words[2, v:v + 1, :] << 7) + (block << 16)
+        shape = words[1, v:v + 1, :]
+        mirrored = 14 * ((shape * 37) >> 8) + 6 - shape
+        code_ref[v:v + 1, :] = mirrored + (words[2, v:v + 1, :] << 7) + (block << 16)
         blocks.append(block)
     for v in range(V):
         @pl.loop(0, E // 16)
@@ -140,6 +141,10 @@
         for cc in range(4):
             own[k, r, :, cc * 8:cc * 8 + 8, :] = total[128:, cc * N:(cc + 1) * N].reshape(16, 8, N)
 
+    def straight(k, r, i):
+        g, way = pl.ds(i * 4, 4), 0 if r == 1 else 1
+        send(own.at[k, r, g], s2.at[k, way, g], s2_s, d2_r.at[k, i], place(k, r, 0, 0))
+
     def chip_sum(k, r):
         got(take.at[k, r], g_s, g_r.at[k, r])
         own[k, r] = own[k, r] + take[k, r]
@@ -147,19 +152,15 @@
         if r == 2:
             for i in (1, 2, 0, 3):
                 send(own.at[k, 2, pl.ds(i * 4, 4)], s1.at[k, i], s1_s, s1_r.at[k, i], up if i < 2 else down)
-        if r == 1:
-            send(own.at[k, 1, pl.ds(8, 8)], s2.at[k, 0, pl.ds(8, 8)], s2_s, d2_r.at[k, 0], up)
-        if r == 3:
-            send(own.at[k, 3, pl.ds(0, 8)], s2.at[k, 1, pl.ds(0, 8)], s2_s, d2_r.at[k, 1], down)
+        if r in (1, 3):
+            straight(k, r, 2 if r == 1 else 1)
 
     steps = [(k, r) for r in (2, 1, 3, 0) for k in range(3)]
-    lag = 2
+    lag = 3
     for n, (k, r) in enumerate(steps):
         partial(k, r)
-        if n >= lag:
+        if n >= lag and steps[n - lag][1] != 0:
             chip_sum(*steps[n - lag])
-    for k, r in steps[len(steps) - lag:]:
-        chip_sum(k, r)
     for i in (1, 2, 0, 3):
         g = pl.ds(i * 4, 4)
         for k in range(3):
@@ -167,13 +168,15 @@
             got(s1.at[k, i], s1_s, s1_r.at[k, i])
             own[k, r, g] = own[k, r, g] + s1[k, i]
             send(own.at[k, r, g], s2.at[k, way, g], s2_s, s2_r.at[k, i], place(k, r, 0, 0))
+            if i in (1, 2):
+                straight(k, r, 0 if r == 3 else 3)
+    for k in range(3):
+        chip_sum(k, 0)
     far_first = sorted(range(1, 16), key=lambda q: -(HOPS[q // 4] + HOPS[q % 4]))
     for i in (1, 2, 0, 3):
         g = pl.ds(i * 4, 4)
         for k in range(3):
-            if i == 1:
-                got(s2.at[k, 0, pl.ds(8, 8)], s2_s, d2_r.at[k, 0])
-                got(s2.at[k, 1, pl.ds(0, 8)], s2_s, d2_r.at[k, 1])
+            got(s2.at[k, 1 if i < 2 else 0, g], s2_s, d2_r.at[k, i])
             got(s2.at[k, 0 if i < 2 else 1, g], s2_s, s2_r.at[k, i])
             own[k, 0, g] = own[k, 0, g] + s2[k, 0, g] + s2[k, 1, g]
             for q in far_first:
@@ -279,26 +282,26 @@
     vmem = pl.BlockSpec(memory_space=pltpu.VMEM)
     return pl.pallas_call(
         main_kernel,
-        out_shape=(jax.ShapeDtypeStruct((C, 1, 8, N), f32), jax.ShapeDtypeStruct((TILES * C + 16, N), f32), jax.ShapeDtypeStruct((V, T), i32)),
+        out_shape=(jax.ShapeDtypeStruct((C, 1, 8, N), f32), jax.ShapeDtypeStruct((TILES * C + 16, N), f32), jax.ShapeDtypeStruct((V, T), i32),
+                   jax.ShapeDtypeStruct((S, N, N), bf16)),
         grid_spec=pltpu.PrefetchScalarGridSpec(
             num_scalar_prefetch=0, grid=(),
             in_specs=[pl.BlockSpec(memory_space=pltpu.HBM)] * len(arrays),
-            out_specs=(vmem, vmem, vmem),
+            out_specs=(vmem, vmem, vmem, vmem),
             scratch_shapes=[
                 pltpu.SMEM((V, T), i32), pltpu.SMEM((V, T), i32), pltpu.VMEM((1, V), i32), pltpu.VMEM((V, 1, T), i32), pltpu.VMEM((3, V, T), i32),
-                pltpu.VMEM((V, C, E, N), bf16), pltpu.VMEM((3, C, 1, 8, N), f32), pltpu.VMEM((12, 136, N), f32), pltpu.VMEM((S, N, N), bf16),
+                pltpu.VMEM((V, C, E, N), bf16), pltpu.VMEM((3, C, 1, 8, N), f32), pltpu.VMEM((12, 136, N), f32),
                 pltpu.VMEM((V * E * C + 16, N), f32), pltpu.VMEM((FWD_UNROLL * 16, N), f32), pltpu.VMEM((TILES, C * N), bf16),
                 pltpu.VMEM((3, 4, 16, 32, N), f32), pltpu.VMEM((3, 4, 16, 32, N), f32), pltpu.VMEM((3, 4, 16, 32, N), f32),
                 pltpu.VMEM((3, 4, 4, 32, N), f32), pltpu.VMEM((3, 2, 16, 32, N), f32), pltpu.VMEM((3, 15, 32, N), f32),
                 pltpu.VMEM((1, N), f32), pltpu.VMEM((128, 1, N), f32), pltpu.VMEM((3, 2, 4, 16, 32, N), bf16),
-            ] + [dma, dma((7,)), dma((3,))] + [dma] * 9 + [dma((3, 4)), dma((3, 4)), dma((3, 4)), dma((3, 2)), dma((3,)), dma, dma((3, 4)), dma((3, 4, 2)), dma((3, 4)), dma((3, 4, 4))]),
+            ] + [dma, dma((7,)), dma((3,))] + [dma] * 9 + [dma((3, 4)), dma((3, 4)), dma((3, 4)), dma((3, 4)), dma((3,)), dma, dma((3, 4)), dma((3, 4, 2)), dma((3, 4)), dma((3, 4, 4))]),
         compiler_params=pltpu.CompilerParams(vmem_limit_bytes=44 << 20, collective_id=0, has_side_effects=True),
         name="main",
     )(*(pltpu.with_memory_space_constraint(v, pltpu.HBM) for v in arrays))
 
 
-def bwd_kernel(code, xs, dir_ref, out_ref, dir_out, ext, table, acc0, acc1, stage, sem):
-    fill_tables(ext, table, True)
+def bwd_kernel(code, xs, table, dir_ref, out_ref, dir_out, acc0, acc1, stage, sem):
     zero = jnp.zeros((64, N), jnp.float32)
 
     @pl.loop(0, (E * C) // 64)
@@ -337,27 +340,26 @@
         leave(n).wait()
 
 
-def backward(code, dirs, direction):
+def backward(code, dirs, table, direction):
     f32 = jnp.float32
     return pl.pallas_call(
         bwd_kernel,
         out_shape=(jax.ShapeDtypeStruct((V, C, E, N), f32), jax.ShapeDtypeStruct((C, 1, 8, N), f32)),
         grid_spec=pltpu.PrefetchScalarGridSpec(
             num_scalar_prefetch=1, grid=(),
-            in_specs=[pl.BlockSpec(memory_space=pltpu.VMEM)] * 2,
+            in_specs=[pl.BlockSpec(memory_space=pltpu.VMEM)] * 3,
             out_specs=(pl.BlockSpec(memory_space=pl.ANY), pl.BlockSpec(memory_space=pltpu.VMEM)),
-            scratch_shapes=[pltpu.VMEM((12, 136, N), f32), pltpu.VMEM((S, N, N), jnp.bfloat16),
-                            pltpu.VMEM((E * C + 16, N), f32), pltpu.VMEM((E * C + 16, N), f32),
+            scratch_shapes=[pltpu.VMEM((E * C + 16, N), f32), pltpu.VMEM((E * C + 16, N), f32),
                             pltpu.VMEM((8, C, 64, N), f32), pltpu.SemaphoreType.DMA((8,))]),
         compiler_params=pltpu.CompilerParams(vmem_limit_bytes=44 << 20),
         name="bwd",
-    )(code, dirs, direction)
+    )(code, dirs, table, direction)
 
 
 def body(kernels, tile_owner, tile_source, tile_target, tile_seed, tile_count, prev_gradient, prev_step, precond):
-    direction, dirs, code = main(tile_count.reshape(1, V), kernels, tile_owner.reshape(V, 1, T), tile_target, tile_seed, tile_source,
+    direction, dirs, code, table = main(tile_count.reshape(1, V), kernels, tile_owner.reshape(V, 1, T), tile_target, tile_seed, tile_source,
                                  prev_gradient, prev_step, precond)
-    event_direction, direction = backward(code, dirs, direction)
+    event_direction, direction = backward(code, dirs, table, direction)
     return direction, event_direction
 
 

time: 74.4 us -> 76 us (1.022)
  Pallas kernels: 73.7 us -> 75.2 us
    pallas_call x1, Pallas kernels: 60.6 us -> 62.6 us  [main(): pl.pallas_call(main_kernel, out_shape=(jax.ShapeDtypeStruct((C, 1, 8, N),...]
where the time goes in v6:
time: 76 us; the launch traced here: 75.8 us
  Pallas kernels  75.2 us (99%)
    pallas_call x1, Pallas kernels, main(): pl.pallas_call(main_kernel, out_shape=(jax.ShapeDtypeStruct((C, 1, 8, N),...  62.6 us
    pallas_call x1, Pallas kernels, backward(): pl.pallas_call(bwd_kernel, out_shape=(jax.ShapeDtypeStruct((V, C, E, N),...  12.6 us

profile of v6, /device:TPU:1, one launch (start us, length us, event | category | flops | bytes accessed | tf_op | source)
XLA Modules:
  0.0 75.8 jit_solution(4107875523043242430)
XLA Ops:
  0.6 62.6 %main.1 = (f32[12,1,8,128]{3,2,1,0:T(8,128)S(1)}, f32[12304,128]{1,0:T(8,128)S(1)}, s32[2,512]{1,0:T(2,128)S(1)}, bf16[84,128,128]{2,1,0:T(8,128)(2,1)S(1)}) custom-call(s32[1,2]{1,0:T(1,128)} %bitcast.3, bf16[2,12,256,128]{3,2,1,0:T(8,128)(2,1)} %kern_hbm.1, s32[2,1,512]{2,1,0:T(1,128)} %bitcast.2, s32[2,512]{1,0:T(2,128)} %target_hbm.1, ...), custom_call_target="tpu_custom_call" | custom-call | tf_op jit(solution)/shard_map/main/pallas_call | solution.py:283
  63.2 12.6 %bwd.1 = (f32[2,12,256,128]{3,2,1,0:T(8,128)}, f32[12,1,8,128]{3,2,1,0:T(8,128)}) custom-call(s32[2,512]{1,0:T(2,128)S(1)} %get-tuple-element.8.code, f32[12304,128]{1,0:T(8,128)S(1)} %get-tuple-element.9.xs, bf16[84,128,128]{2,1,0:T(8,128)(2,1)S(1)} %get-tuple-element.10.table, f32[12,1,8,128]{3,2,1,0:T(8,128)S(1)} %get-tuple-element.11.dir_ref), custom_call_target="tpu_custom_call" | custom-call | tf_op jit(solution)/shard_map/bwd/pallas_call | solution.py:345

commit v7 on v6

--- a/solution.py
+++ b/solution.py
@@ -141,10 +141,6 @@
         for cc in range(4):
             own[k, r, :, cc * 8:cc * 8 + 8, :] = total[128:, cc * N:(cc + 1) * N].reshape(16, 8, N)
 
-    def straight(k, r, i):
-        g, way = pl.ds(i * 4, 4), 0 if r == 1 else 1
-        send(own.at[k, r, g], s2.at[k, way, g], s2_s, d2_r.at[k, i], place(k, r, 0, 0))
-
     def chip_sum(k, r):
         got(take.at[k, r], g_s, g_r.at[k, r])
         own[k, r] = own[k, r] + take[k, r]
@@ -152,15 +148,19 @@
         if r == 2:
             for i in (1, 2, 0, 3):
                 send(own.at[k, 2, pl.ds(i * 4, 4)], s1.at[k, i], s1_s, s1_r.at[k, i], up if i < 2 else down)
-        if r in (1, 3):
-            straight(k, r, 2 if r == 1 else 1)
+        if r == 1:
+            send(own.at[k, 1, pl.ds(8, 8)], s2.at[k, 0, pl.ds(8, 8)], s2_s, d2_r.at[k, 0], up)
+        if r == 3:
+            send(own.at[k, 3, pl.ds(0, 8)], s2.at[k, 1, pl.ds(0, 8)], s2_s, d2_r.at[k, 1], down)
 
     steps = [(k, r) for r in (2, 1, 3, 0) for k in range(3)]
-    lag = 3
+    lag = 2
     for n, (k, r) in enumerate(steps):
         partial(k, r)
-        if n >= lag and steps[n - lag][1] != 0:
+        if n >= lag:
             chip_sum(*steps[n - lag])
+    for k, r in steps[len(steps) - lag:]:
+        chip_sum(k, r)
     for i in (1, 2, 0, 3):
         g = pl.ds(i * 4, 4)
         for k in range(3):
@@ -168,15 +168,13 @@
             got(s1.at[k, i], s1_s, s1_r.at[k, i])
             own[k, r, g] = own[k, r, g] + s1[k, i]
             send(own.at[k, r, g], s2.at[k, way, g], s2_s, s2_r.at[k, i], place(k, r, 0, 0))
-            if i in (1, 2):
-                straight(k, r, 0 if r == 3 else 3)
-    for k in range(3):
-        chip_sum(k, 0)
     far_first = sorted(range(1, 16), key=lambda q: -(HOPS[q // 4] + HOPS[q % 4]))
     for i in (1, 2, 0, 3):
         g = pl.ds(i * 4, 4)
         for k in range(3):
-            got(s2.at[k, 1 if i < 2 else 0, g], s2_s, d2_r.at[k, i])
+            if i == 1:
+                got(s2.at[k, 0, pl.ds(8, 8)], s2_s, d2_r.at[k, 0])
+                got(s2.at[k, 1, pl.ds(0, 8)], s2_s, d2_r.at[k, 1])
             got(s2.at[k, 0 if i < 2 else 1, g], s2_s, s2_r.at[k, i])
             own[k, 0, g] = own[k, 0, g] + s2[k, 0, g] + s2[k, 1, g]
             for q in far_first:
@@ -295,7 +293,7 @@
                 pltpu.VMEM((3, 4, 16, 32, N), f32), pltpu.VMEM((3, 4, 16, 32, N), f32), pltpu.VMEM((3, 4, 16, 32, N), f32),
                 pltpu.VMEM((3, 4, 4, 32, N), f32), pltpu.VMEM((3, 2, 16, 32, N), f32), pltpu.VMEM((3, 15, 32, N), f32),
                 pltpu.VMEM((1, N), f32), pltpu.VMEM((128, 1, N), f32), pltpu.VMEM((3, 2, 4, 16, 32, N), bf16),
-            ] + [dma, dma((7,)), dma((3,))] + [dma] * 9 + [dma((3, 4)), dma((3, 4)), dma((3, 4)), dma((3, 4)), dma((3,)), dma, dma((3, 4)), dma((3, 4, 2)), dma((3, 4)), dma((3, 4, 4))]),
+            ] + [dma, dma((7,)), dma((3,))] + [dma] * 9 + [dma((3, 4)), dma((3, 4)), dma((3, 4)), dma((3, 2)), dma((3,)), dma, dma((3, 4)), dma((3, 4, 2)), dma((3, 4)), dma((3, 4, 4))]),
         compiler_params=pltpu.CompilerParams(vmem_limit_bytes=44 << 20, collective_id=0, has_side_effects=True),
         name="main",
     )(*(pltpu.with_memory_space_constraint(v, pltpu.HBM) for v in arrays))

time: 76 us -> 74.1 us (0.975)
  Pallas kernels: 75.2 us -> 73.3 us
    pallas_call x1, Pallas kernels: 62.6 us -> 60.7 us  [main(): pl.pallas_call(main_kernel, out_shape=(jax.ShapeDtypeStruct((C, 1, 8, N),...]
where the time goes in v7:
time: 74.1 us; the launch traced here: 74 us
  Pallas kernels  73.3 us (99%)
    pallas_call x1, Pallas kernels, main(): pl.pallas_call(main_kernel, out_shape=(jax.ShapeDtypeStruct((C, 1, 8, N),...  60.7 us
    pallas_call x1, Pallas kernels, backward(): pl.pallas_call(bwd_kernel, out_shape=(jax.ShapeDtypeStruct((V, C, E, N),...  12.7 us

profile of v7, /device:TPU:1, one launch (start us, length us, event | category | flops | bytes accessed | tf_op | source)
XLA Modules:
  0.0 74.0 jit_solution(11327798212818234334)
XLA Ops:
  0.6 60.7 %main.1 = (f32[12,1,8,128]{3,2,1,0:T(8,128)S(1)}, f32[12304,128]{1,0:T(8,128)S(1)}, s32[2,512]{1,0:T(2,128)S(1)}, bf16[84,128,128]{2,1,0:T(8,128)(2,1)S(1)}) custom-call(s32[1,2]{1,0:T(1,128)} %bitcast.3, bf16[2,12,256,128]{3,2,1,0:T(8,128)(2,1)} %kern_hbm.1, s32[2,1,512]{2,1,0:T(1,128)} %bitcast.2, s32[2,512]{1,0:T(2,128)} %target_hbm.1, ...), custom_call_target="tpu_custom_call" | custom-call | tf_op jit(solution)/shard_map/main/pallas_call | solution.py:281
  61.3 12.7 %bwd.1 = (f32[2,12,256,128]{3,2,1,0:T(8,128)}, f32[12,1,8,128]{3,2,1,0:T(8,128)}) custom-call(s32[2,512]{1,0:T(2,128)S(1)} %get-tuple-element.8.code, f32[12304,128]{1,0:T(8,128)S(1)} %get-tuple-element.9.xs, bf16[84,128,128]{2,1,0:T(8,128)(2,1)S(1)} %get-tuple-element.10.table, f32[12,1,8,128]{3,2,1,0:T(8,128)S(1)} %get-tuple-element.11.dir_ref), custom_call_target="tpu_custom_call" | custom-call | tf_op jit(solution)/shard_map/bwd/pallas_call | solution.py:343
